TPU v7x, 256 devices: a whole 4x4x8 slice. The times are simulated.
256 devices in a mesh: tp: 32 (over z, y), dp: 8 (over x, core).
Axes of the slice: x: 4, y: 4, z: 8, core: 2. Of those that a mesh axis runs over, the one named last changes fastest.
Arguments:
- hidden_in: bfloat16 [8192, 2048], P('dp')
- targets: bfloat16 [8192, 2048], P('dp')
- w_up: bfloat16 [4, 2048, 8192], P(None, None, 'tp')
- w_down: bfloat16 [4, 8192, 2048], P(None, 'tp')
Outputs:
- output 1: float32 [4, 2048, 8192], P(None, None, 'tp')
- output 2: float32 [4, 8192, 2048], P(None, 'tp')
All inputs are finite; a program needn't handle non-finite values.
Results may differ from a plain program's by a relative error of at most 0.0111594.
Values are sent between devices in bfloat16 or wider.
A program may use at most 768 MiB of HBM per device.

v0:
```python
import functools
import jax
import jax.numpy as jnp
from jax import lax
from jax.sharding import PartitionSpec as P

ROW_CONTRACT = (((0,), (0,)), ((), ()))
COL_CONTRACT = (((1,), (1,)), ((), ()))


def gelu_tanh(value):
    return jax.nn.gelu(value, approximate=True)


def local_step(hidden, targets, w_up, w_down, total_tokens):
    layers = w_up.shape[0]
    h_cur = hidden
    saved = []
    for layer in range(layers):
        pre_act = jnp.dot(h_cur, w_up[layer], preferred_element_type=jnp.float32).astype(jnp.bfloat16)
        act_val = gelu_tanh(pre_act.astype(jnp.float32)).astype(jnp.bfloat16)
        part_out = jnp.dot(act_val, w_down[layer], preferred_element_type=jnp.float32)
        branch = lax.psum(part_out, "tp").astype(jnp.bfloat16)
        saved.append((h_cur, pre_act, act_val))
        h_cur = h_cur + branch
    err_f32 = (h_cur.astype(jnp.float32) - targets.astype(jnp.float32)) / total_tokens
    g_cur = err_f32.astype(jnp.bfloat16)
    grads_up = [None] * layers
    grads_down = [None] * layers
    for layer in reversed(range(layers)):
        h_in, pre_act, act_val = saved[layer]
        g_down = lax.dot_general(act_val, g_cur, ROW_CONTRACT, preferred_element_type=jnp.float32)
        grads_down[layer] = lax.psum(g_down, "dp")
        d_act = lax.dot_general(g_cur, w_down[layer], COL_CONTRACT, preferred_element_type=jnp.float32)
        _, gelu_vjp = jax.vjp(gelu_tanh, pre_act.astype(jnp.float32))
        d_pre = gelu_vjp(d_act)[0].astype(jnp.bfloat16)
        g_up = lax.dot_general(h_in, d_pre, ROW_CONTRACT, preferred_element_type=jnp.float32)
        grads_up[layer] = lax.psum(g_up, "dp")
        if layer > 0:
            back_part = lax.dot_general(d_pre, w_up[layer], COL_CONTRACT, preferred_element_type=jnp.float32)
            g_cur = (g_cur.astype(jnp.float32) + lax.psum(back_part, "tp")).astype(jnp.bfloat16)
    return jnp.stack(grads_up), jnp.stack(grads_down)


def solution(mesh):
    def grad_step(hidden_in, targets, w_up, w_down):
        step_fn = functools.partial(local_step, total_tokens=hidden_in.shape[0])
        mapped = jax.shard_map(step_fn, mesh=mesh, in_specs=(P("dp", None), P("dp", None), P(None, None, "tp"), P(None, "tp", None)), out_specs=(P(None, None, "tp"), P(None, "tp", None)), check_vma=False)
        return mapped(hidden_in, targets, w_up, w_down)

    return grad_step
```

profile of v0, /device:TPU:1, one launch (start us, length us, event | category | flops | bytes accessed | tf_op | source)
XLA Modules:
  0.0 1755.0 jit_solution(7295288952746475682)
XLA Ops:
  7.2 0.0 all-reduce.10.cloned.1.call-start
  7.2 3.7 convolution_convert_fusion.3
  10.9 6.0 fusion.63
  17.0 195.3 %all-reduce.17 = bf16[1024,2048]{1,0:T(8,128)(2,1)} all-reduce(f32[1024,2048]{1,0:T(8,128)} %fusion.63), channel_id=1, replica_groups=mesh['tp'=32,'dp'=8] {'tp'}, use_global_device_ids=true, to_apply=%region_0.0 | all-reduce | flops 2097152 | bytes 12582912 | tf_op jit(solution)/shard_map/psum | solution.py:23
  212.2 5.4 add.178
  217.6 2.0 copy-done
  219.6 2.5 convolution_convert_fusion.2
  222.1 6.0 fusion.56
  228.1 186.1 %all-reduce.18 = bf16[1024,2048]{1,0:T(8,128)(2,1)} all-reduce(f32[1024,2048]{1,0:T(8,128)} %fusion.56), channel_id=1, replica_groups=mesh['tp'=32,'dp'=8] {'tp'}, use_global_device_ids=true, to_apply=%region_1.0 | all-reduce | flops 2097152 | bytes 12582912 | tf_op jit(solution)/shard_map/psum | solution.py:23
  414.3 5.4 add.177
  419.7 1.9 copy-done.2
  421.6 2.5 convolution_convert_fusion.1
  424.1 6.0 fusion.49
  430.1 183.8 %all-reduce.19 = bf16[1024,2048]{1,0:T(8,128)(2,1)} all-reduce(f32[1024,2048]{1,0:T(8,128)} %fusion.49), channel_id=1, replica_groups=mesh['tp'=32,'dp'=8] {'tp'}, use_global_device_ids=true, to_apply=%region_2.0 | all-reduce | flops 2097152 | bytes 12582912 | tf_op jit(solution)/shard_map/psum | solution.py:23
  613.9 5.4 add.176
  619.3 1.9 copy-done.4
  621.2 2.5 convolution_convert_fusion
  623.7 6.0 fusion.42
  629.7 181.9 %all-reduce.20 = bf16[1024,2048]{1,0:T(8,128)(2,1)} all-reduce(f32[1024,2048]{1,0:T(8,128)} %fusion.42), channel_id=1, replica_groups=mesh['tp'=32,'dp'=8] {'tp'}, use_global_device_ids=true, to_apply=%region_3.0 | all-reduce | flops 2097152 | bytes 12582912 | tf_op jit(solution)/shard_map/psum | solution.py:23
  811.6 7.7 multiply_convert_fusion
  819.3 3.8 fusion.6
  823.1 5.9 fusion.44
  829.0 0.0 all-reduce.12.cloned.1.call-start
  829.0 239.0 %all-reduce.10.cloned.1.call-done = f32[1024,2048]{1,0:T(8,128)} async-done(((f32[1024,2048]{1,0:T(8,128)}), f32[1024,2048]{1,0:T(8,128)}) %all-reduce.10.cloned.1.call-update) | async-done | bytes 8388624 | tf_op jit(solution)/shard_map/psum | solution.py:41
  1068.1 6.1 add_convert_fusion.2
  1074.2 3.8 fusion.9
  1078.0 5.9 fusion.51
  1083.9 0.0 all-reduce.12.cloned.1.call-update
  1083.9 0.0 all-reduce.14.cloned.1.call-start
  1083.9 210.3 %all-reduce.12.cloned.1.call-done = f32[1024,2048]{1,0:T(8,128)} async-done(((f32[1024,2048]{1,0:T(8,128)}), f32[1024,2048]{1,0:T(8,128)}) %all-reduce.12.cloned.1.call-update) | async-done | bytes 8388624 | tf_op jit(solution)/shard_map/psum | solution.py:41
  1294.2 6.1 add_convert_fusion.1
  1300.3 3.8 fusion.12
  1304.1 0.8 copy-done.12
  1304.9 5.9 fusion.58
  1310.8 0.2 all-reduce.16.cloned.1.call-start
  1311.1 5.0 convolution_bitcast_fusion.4
  1316.0 2.7 convolution_bitcast_fusion
  1318.8 2.6 convolution_bitcast_fusion.5
  1321.4 2.8 convolution_bitcast_fusion.1
  1324.2 2.6 convolution_bitcast_fusion.6
  1326.8 2.7 convolution_bitcast_fusion.2
  1329.5 191.8 %all-reduce.14.cloned.1.call-done = f32[1024,2048]{1,0:T(8,128)} async-done(((f32[1024,2048]{1,0:T(8,128)}), f32[1024,2048]{1,0:T(8,128)}) %all-reduce.14.cloned.1.call-update) | async-done | bytes 8388624 | tf_op jit(solution)/shard_map/psum | solution.py:41
  1521.3 7.3 convolution_bitcast_fusion.3
  1528.6 12.4 convolution_bitcast_fusion.7
  1541.0 186.7 %all-reduce.16.cloned.1.call-done = (f32[1,2048,256]{1,2,0:T(8,128)}, f32[1,2048,256]{1,2,0:T(8,128)}, f32[1,2048,256]{1,2,0:T(8,128)}, f32[1,2048,256]{1,2,0:T(...) async-done(((f32[1,2048,256]{1,2,0:T(8,128)}, f32[1,2048,256]{1,2,0:T(8,128)}, ...) | async-done | bytes 16777232 | tf_op jit(solution)/shard_map/psum | solution.py:38
  1727.7 6.1 pad_maximum_fusion
  1733.8 8.8 copy.9
  1742.6 5.7 pad_maximum_fusion.1
  (27 shorter events, 0.1 us)
Async XLA Ops:
  7.2 1060.9 %all-reduce.10.cloned.1.call-start = ((), (), s32[]{:S(2)}) async-start(), calls=%async_computation | async-start | bytes 16777216 | tf_op jit(solution)/shard_map/psum | solution.py:41
  217.6 2.0 copy-start
  419.7 1.9 copy-start.2
  619.3 1.9 copy-start.4
  819.3 3.8 copy-start.5
  829.0 465.2 %all-reduce.12.cloned.1.call-start = ((), (), s32[]{:S(2)}) async-start(), calls=%async_computation.1 | async-start | bytes 16777216 | tf_op jit(solution)/shard_map/psum | solution.py:41
  1074.1 3.8 copy-start.7
  1083.9 437.4 %all-reduce.14.cloned.1.call-start = ((), (), s32[]{:S(2)}) async-start(), calls=%async_computation.2 | async-start | bytes 16777216 | tf_op jit(solution)/shard_map/psum | solution.py:41
  1300.3 3.8 copy-start.9
  1304.1 0.8 copy-start.12
  1310.8 416.9 %all-reduce.16.cloned.1.call-start = ((), (), s32[]{:S(2)}) async-start(), calls=%async_computation.3 | async-start | bytes 33554432 | tf_op jit(solution)/shard_map/psum | solution.py:38
  1311.0 5.0 copy-start.6
  1316.0 2.8 copy-start.3
  1318.8 2.6 copy-start.8
  1321.4 2.8 copy-start.1
  1321.4 2.8 copy-start.13
  1324.2 2.6 copy-start.10
  1733.8 8.8 copy-start.11
Sparse Core Ops, SparseCore 0:
  829.1 238.9 all-reduce.9
  1084.0 210.1 all-reduce.11
  1310.9 210.3 all-reduce.13
  1541.2 186.5 all-reduce.15
where the time goes:
time: 1760 us
  waiting for transfers between devices  828 us (47%)
  blocking collectives  747 us (42%)
  matrix products  102 us (6%)
  other arithmetic  47.7 us (3%)
    psum x4, blocking collectives, local_step(): branch = lax.psum(part_out, 'tp').astype(jnp.bfloat16)  747 us
    psum x3, waiting for transfers between devices, local_step(): lax.psum(back_part, 'tp')  641 us
    psum x1, waiting for transfers between devices, local_step(): grads_up[layer] = lax.psum(g_up, 'dp')  187 us
  transfers between devices with their start and end apart: 4, of which 4 were waited for; matrix products, arithmetic and copies ran while one was open for 1% of the time, Pallas kernels for 0%

commit v1 on v0

v1 whole, which is shorter than its diff:
```python
import functools
import jax
import jax.numpy as jnp
from jax import lax
from jax.experimental import pallas as pl
from jax.experimental.pallas import tpu as pltpu
from jax.sharding import PartitionSpec as P

NZ = 8
NY = 4
ROW_CONTRACT = (((0,), (0,)), ((), ()))
COL_CONTRACT = (((1,), (1,)), ((), ()))
CHAINS = ((0, 0, 4), (1, 0, 3), (1, 1, 4), (0, 1, 3))
ANY = pl.BlockSpec(memory_space=pl.ANY)
VMEM = pl.BlockSpec(memory_space=pltpu.VMEM)


def gelu_tanh(value):
    return jax.nn.gelu(value, approximate=True)


def place():
    tp = lax.axis_index("tp")
    return lax.div(tp, NY), lax.rem(tp, NY)


def entry_barrier(z, y, with_z):
    peers = [(z, lax.rem(y + s, NY)) for s in (1, 2, 3)]
    if with_z:
        peers += [(lax.rem(z + 1, NZ), y), (lax.rem(z + NZ - 1, NZ), y)]
    sem = pltpu.get_barrier_semaphore()
    for pz, py in peers:
        pl.semaphore_signal(sem, inc=1, device_id={"tp": pz * NY + py}, device_id_type=pl.DeviceIdType.MESH)
    pl.semaphore_wait(sem, len(peers))


def remote(src, dst, send_sem, recv_sem, pz, py):
    return pltpu.make_async_remote_copy(
        src_ref=src, dst_ref=dst, send_sem=send_sem, recv_sem=recv_sem,
        device_id={"tp": pz * NY + py}, device_id_type=pl.DeviceIdType.MESH)


class RowGather:
    def __init__(self, block, out, z, y, local_sem, send_sem, recv_sem):
        rows = block.shape[0]
        half = rows // 2
        up, down = lax.rem(y + 1, NY), lax.rem(y + NY - 1, NY)
        own = out.at[pl.ds(pl.multiple_of(y * rows, rows), rows)]
        lower = out.at[pl.ds(pl.multiple_of(down * rows, rows), half)]
        upper = out.at[pl.ds(pl.multiple_of(up * rows + half, half), half)]
        self.local = pltpu.make_async_copy(block, own, local_sem)
        self.first = [remote(block, own, send_sem.at[0], recv_sem.at[0], z, up),
                      remote(block, own, send_sem.at[1], recv_sem.at[1], z, down)]
        self.second = [remote(lower, lower, send_sem.at[2], recv_sem.at[2], z, up),
                       remote(upper, upper, send_sem.at[3], recv_sem.at[3], z, down)]

    def start(self):
        self.local.start()
        for copy in self.first:
            copy.start()

    def relay(self):
        for copy, onward in zip(self.first, self.second):
            copy.wait_recv()
            onward.start()

    def finish(self):
        self.local.wait()
        for copy in self.first:
            copy.wait_send()
        for copy in self.second:
            copy.wait()


class ColumnExchange:
    def __init__(self, block, out, z, y, local_sem, send_sem, recv_sem):
        rows, cols = block.shape[0], block.shape[1] // NY
        own = out.at[pl.ds(pl.multiple_of(y * rows, rows), rows)]

        def columns(index):
            return block.at[:, pl.ds(pl.multiple_of(index * cols, cols), cols)]

        self.local = pltpu.make_async_copy(columns(y), own, local_sem)
        self.copies = []
        for s in (1, 2, 3):
            dest = lax.rem(y + s, NY)
            self.copies.append(remote(columns(dest), own, send_sem.at[s - 1], recv_sem.at[s - 1], z, dest))

    def start(self):
        self.local.start()
        for copy in self.copies:
            copy.start()

    def finish(self):
        self.local.wait()
        for copy in self.copies:
            copy.wait()


class SumGather:
    def __init__(self, part, slots, out, z, y, send_sem, recv_sem):
        self.part, self.slots, self.out, self.z, self.y = part, slots, out, z, y
        self.send_sem, self.recv_sem = send_sem, recv_sem
        self.rows, self.cols = part.shape[0] // NZ, part.shape[1] // 2
        self.copies = []
        self.last = {}

    def block(self, ref, owner, half):
        return ref.at[pl.ds(pl.multiple_of(owner * self.rows, self.rows), self.rows), pl.ds(half * self.cols, self.cols)]

    def shifted(self, direction, amount):
        return lax.rem(self.z + (amount if direction == 0 else NZ - amount), NZ)

    def send(self, index, src, dst, direction):
        copy = remote(src, dst, self.send_sem.at[index], self.recv_sem.at[index], self.shifted(direction, 1), self.y)
        copy.start()
        self.copies.append(copy)
        return copy

    def reduce_step(self, chain, step):
        direction, half, hops = CHAINS[chain]
        mine = self.block(self.part, self.shifted(direction, hops - step), half)
        if step > 0:
            self.last[chain].wait_recv()
            mine[...] = mine[...] + self.slots[chain * 4 + step - 1]
        index = chain * 4 + step
        self.last[chain] = self.send(index, mine, self.slots.at[index], direction)

    def reduce_rest(self):
        for step in (1, 2, 3):
            for chain, (_, _, hops) in enumerate(CHAINS):
                if step < hops:
                    self.reduce_step(chain, step)

    def total(self, half):
        value = self.block(self.part, self.z, half)[...]
        for chain, (_, h, hops) in enumerate(CHAINS):
            if h == half:
                self.last[chain].wait_recv()
                value = value + self.slots[chain * 4 + hops - 1]
        return value

    def gather_step(self, chain, step):
        direction, half, hops = CHAINS[chain]
        if step > 0:
            self.last[chain].wait_recv()
        held = self.block(self.out, self.shifted(1 - direction, step) if step else self.z, half)
        self.last[chain] = self.send(16 + chain * 4 + step, held, held, direction)

    def gather(self, steps):
        for step in steps:
            for chain, (_, _, hops) in enumerate(CHAINS):
                if step < hops:
                    self.gather_step(chain, step)

    def finish(self):
        for copy in self.last.values():
            copy.wait_recv()
        for copy in self.copies:
            copy.wait_send()


def forward_kernel(is_last, gather_h, total_tokens, *refs):
    refs = list(refs)
    h_ref, wu_hbm, wd_hbm = refs[:3]
    refs = refs[3:]
    t_ref = refs.pop(0) if is_last else None
    out_ref, u_ref, a_out = refs[:3]
    refs = refs[3:]
    h_out = refs.pop(0) if gather_h else None
    wu, wd, act, part, slots, wsem, lsem, ysend, yrecv, zsend, zrecv = refs
    blocks = wd_hbm.shape[0]
    ucols = wu.shape[1] // 4
    dcols = wd.shape[1] // blocks
    z, y = place()

    def wu_copy(n):
        cols = pl.ds(pl.multiple_of(n * ucols, ucols), ucols)
        return pltpu.make_async_copy(wu_hbm.at[:, cols], wu.at[:, cols], wsem.at[n])

    def wd_copy(n):
        cols = pl.ds(pl.multiple_of(n * dcols, dcols), dcols)
        return pltpu.make_async_copy(wd_hbm.at[n], wd.at[:, cols], wsem.at[4 + n])

    for n in range(4):
        wu_copy(n).start()
    for n in range(blocks):
        wd_copy(n).start()
    entry_barrier(z, y, True)
    if gather_h:
        rows = RowGather(h_ref, h_out, z, y, lsem.at[1], ysend.at[pl.ds(3, 4)], yrecv.at[pl.ds(3, 4)])
        rows.start()

    @pl.loop(0, 4)
    def _(n):
        wu_copy(n).wait()
        cols = pl.ds(pl.multiple_of(n * ucols, ucols), ucols)
        pre = jnp.dot(h_ref[...], wu[:, cols], preferred_element_type=jnp.float32).astype(jnp.bfloat16)
        u_ref[:, cols] = pre
        act[:, cols] = gelu_tanh(pre.astype(jnp.float32)).astype(jnp.bfloat16)

    sums = SumGather(part, slots, out_ref, z, y, zsend, zrecv)
    exchange = ColumnExchange(act, a_out, z, y, lsem.at[0], ysend.at[pl.ds(0, 3)], yrecv.at[pl.ds(0, 3)])

    def down(n):
        wd_copy(n).wait()
        cols = pl.ds(pl.multiple_of(n * dcols, dcols), dcols)
        part[:, cols] = jnp.dot(act[...], wd[:, cols], preferred_element_type=jnp.float32)

    pl.loop(0, blocks // 2)(down)
    sums.reduce_step(0, 0)
    sums.reduce_step(1, 0)
    pl.loop(blocks // 2, blocks)(down)
    sums.reduce_step(2, 0)
    sums.reduce_step(3, 0)
    exchange.start()
    sums.reduce_rest()
    for half in (0, 1):
        branch = sums.total(half).astype(jnp.bfloat16)
        value = sums.block(h_ref, z, half)[...] + branch
        if is_last:
            half_cols = pl.ds(half * sums.cols, sums.cols)
            err = value.astype(jnp.float32) - t_ref[:, half_cols].astype(jnp.float32)
            value = (err / total_tokens).astype(jnp.bfloat16)
        sums.block(out_ref, z, half)[...] = value
    sums.gather((0, 1))
    if gather_h:
        rows.relay()
    sums.gather((2, 3))
    sums.finish()
    exchange.finish()
    if gather_h:
        rows.finish()


def backward_kernel(has_sum, *refs):
    refs = list(refs)
    g_ref, wd_hbm, u_ref = refs[:3]
    refs = refs[3:]
    wu_hbm = refs.pop(0) if has_sum else None
    out_ref = refs.pop(0) if has_sum else None
    du_out, g_out = refs[:2]
    refs = refs[2:]
    if has_sum:
        wd, dpre, wsem, lsem, ysend, yrecv, wu, part, slots, zsend, zrecv = refs
    else:
        wd, dpre, wsem, lsem, ysend, yrecv = refs
    blocks = wd_hbm.shape[0]
    dcols = wd.shape[1] // blocks
    urows = wd.shape[0] // 4
    z, y = place()

    def wd_copy(n):
        return pltpu.make_async_copy(wd_hbm.at[n], wd.at[:, pl.ds(n * dcols, dcols)], wsem.at[n])

    for n in range(blocks):
        wd_copy(n).start()
    if has_sum:
        wu_copy = pltpu.make_async_copy(wu_hbm, wu, wsem.at[blocks])
        wu_copy.start()
    entry_barrier(z, y, has_sum)
    rows = RowGather(g_ref, g_out, z, y, lsem.at[1], ysend.at[pl.ds(3, 4)], yrecv.at[pl.ds(3, 4)])
    rows.start()
    for n in range(blocks):
        wd_copy(n).wait()

    @pl.loop(0, 4)
    def _(n):
        at = pl.ds(pl.multiple_of(n * urows, urows), urows)
        d_act = lax.dot_general(g_ref[...], wd[at, :], COL_CONTRACT, preferred_element_type=jnp.float32)
        _, gelu_vjp = jax.vjp(gelu_tanh, u_ref[:, at].astype(jnp.float32))
        dpre[:, at] = gelu_vjp(d_act)[0].astype(jnp.bfloat16)

    exchange = ColumnExchange(dpre, du_out, z, y, lsem.at[0], ysend.at[pl.ds(0, 3)], yrecv.at[pl.ds(0, 3)])
    if not has_sum:
        exchange.start()
        rows.relay()
        exchange.finish()
        rows.finish()
        return
    wu_copy.wait()
    sums = SumGather(part, slots, out_ref, z, y, zsend, zrecv)
    tile = wu.shape[0] // 8

    def back(n):
        at = pl.ds(pl.multiple_of(n * tile, tile), tile)
        part[:, at] = lax.dot_general(dpre[...], wu[at, :], COL_CONTRACT, preferred_element_type=jnp.float32)

    pl.loop(0, 4)(back)
    sums.reduce_step(0, 0)
    sums.reduce_step(1, 0)
    pl.loop(4, 8)(back)
    sums.reduce_step(2, 0)
    sums.reduce_step(3, 0)
    exchange.start()
    sums.reduce_rest()
    for half in (0, 1):
        total = sums.total(half)
        sums.block(out_ref, z, half)[...] = (sums.block(g_ref, z, half)[...].astype(jnp.float32) + total).astype(jnp.bfloat16)
    sums.gather((0, 1))
    rows.relay()
    sums.gather((2, 3))
    sums.finish()
    exchange.finish()
    rows.finish()


def params(collective_id):
    return pltpu.CompilerParams(collective_id=collective_id, has_side_effects=True, vmem_limit_bytes=48 * 1024 * 1024)


def sum_scratch(rows, width):
    return [pltpu.VMEM((rows, width), jnp.float32), pltpu.VMEM((16, rows // NZ, width // 2), jnp.float32)]


SUM_SEMS = [pltpu.SemaphoreType.DMA((32,)), pltpu.SemaphoreType.DMA((32,))]
Y_SEMS = [pltpu.SemaphoreType.DMA((2,)), pltpu.SemaphoreType.DMA((7,)), pltpu.SemaphoreType.DMA((7,))]


def forward_block(h_cur, w_up, w_down, targets, gather_h, total_tokens, collective_id):
    rows, width = h_cur.shape
    hidden = w_up.shape[1]
    outs = [jax.ShapeDtypeStruct((rows, width), jnp.bfloat16), jax.ShapeDtypeStruct((rows, hidden), jnp.bfloat16),
            jax.ShapeDtypeStruct((rows * NY, hidden // NY), jnp.bfloat16)]
    out_specs = [VMEM, VMEM, ANY]
    args, in_specs = [h_cur, w_up, w_down], [VMEM, ANY, ANY]
    if targets is not None:
        args.append(targets)
        in_specs.append(VMEM)
    if gather_h:
        outs.append(jax.ShapeDtypeStruct((rows * NY, width), jnp.bfloat16))
        out_specs.append(ANY)
    part, slots = sum_scratch(rows, width)
    return pl.pallas_call(
        functools.partial(forward_kernel, targets is not None, gather_h, total_tokens),
        out_shape=outs, in_specs=in_specs, out_specs=out_specs,
        scratch_shapes=[pltpu.VMEM((width, hidden), jnp.bfloat16), pltpu.VMEM((hidden, width), jnp.bfloat16),
                        pltpu.VMEM((rows, hidden), jnp.bfloat16), part, slots,
                        pltpu.SemaphoreType.DMA((4 + w_down.shape[0],))] + Y_SEMS + SUM_SEMS,
        compiler_params=params(collective_id), name="fwd",
        cost_estimate=pl.CostEstimate(flops=40_000_000_000, bytes_accessed=20_000_000, transcendentals=0),
    )(*args)


def backward_block(g_cur, w_up, w_down, pre_act, has_sum, collective_id):
    rows, width = g_cur.shape
    hidden = w_up.shape[1]
    outs = [jax.ShapeDtypeStruct((rows * NY, hidden // NY), jnp.bfloat16), jax.ShapeDtypeStruct((rows * NY, width), jnp.bfloat16)]
    out_specs = [ANY, ANY]
    args, in_specs = [g_cur, w_down, pre_act], [VMEM, ANY, VMEM]
    scratch = [pltpu.VMEM((hidden, width), jnp.bfloat16), pltpu.VMEM((rows, hidden), jnp.bfloat16),
               pltpu.SemaphoreType.DMA((w_down.shape[0] + 1,))] + Y_SEMS
    if has_sum:
        outs.insert(0, jax.ShapeDtypeStruct((rows, width), jnp.bfloat16))
        out_specs.insert(0, VMEM)
        args.append(w_up)
        in_specs.append(ANY)
        part, slots = sum_scratch(rows, width)
        scratch += [pltpu.VMEM((width, hidden), jnp.bfloat16), part, slots] + SUM_SEMS
    return pl.pallas_call(
        functools.partial(backward_kernel, has_sum),
        out_shape=outs, in_specs=in_specs, out_specs=out_specs, scratch_shapes=scratch,
        compiler_params=params(collective_id), name="bwd",
        cost_estimate=pl.CostEstimate(flops=40_000_000_000, bytes_accessed=20_000_000, transcendentals=0),
    )(*args)


def gather_weights(up_piece, down_piece):
    groups = [[z * NY + y for y in range(NY)] for z in range(NZ)]
    both = lax.all_gather(jnp.stack([up_piece, down_piece]), "tp", axis_index_groups=groups)
    ny, _, _, cols = both.shape
    up = both[:, 0].transpose(1, 0, 2).reshape(up_piece.shape[0], ny * up_piece.shape[1])
    down = both[:, 1].reshape(ny * down_piece.shape[0], down_piece.shape[1])
    return lax.all_gather(up, "dp", axis=0, tiled=True), lax.all_gather(down, "dp", axis=0)


def local_step(hidden, targets, w_up, w_down, n_dp):
    layers, width, cols = w_up.shape
    tp, dp = lax.axis_index("tp"), lax.axis_index("dp")
    z, y = lax.div(tp, NY), lax.rem(tp, NY)
    rows = hidden.shape[0] // NY
    piece = width // n_dp
    weights = []
    for layer in range(layers):
        up_piece = lax.dynamic_slice(w_up[layer], (dp * piece, 0), (piece, cols))
        down_piece = lax.dynamic_slice(w_down[layer], (0, dp * piece), (cols, piece))
        weights.append(gather_weights(up_piece, down_piece))
    h_cur = lax.dynamic_slice(hidden, (y * rows, 0), (rows, width))
    t_own = lax.dynamic_slice(targets, (y * rows + z * (rows // NZ), 0), (rows // NZ, width))
    saved = []
    h_all = [hidden]
    for layer in range(layers):
        last = layer == layers - 1
        outs = forward_block(h_cur, *weights[layer], t_own if last else None, layer > 0, hidden.shape[0] * n_dp, layer)
        h_cur, pre_act, act_all = outs[:3]
        if layer > 0:
            h_all.append(outs[3])
        saved.append((pre_act, act_all))
    g_cur = h_cur
    grads_up, grads_down = [None] * layers, [None] * layers
    for layer in reversed(range(layers)):
        pre_act, act_all = saved[layer]
        outs = backward_block(g_cur, *weights[layer], pre_act, layer > 0, layers + layer)
        if layer > 0:
            g_cur = outs[0]
        du_all, g_all = outs[-2:]
        g_down = lax.dot_general(act_all, g_all, ROW_CONTRACT, preferred_element_type=jnp.float32)
        g_up = lax.dot_general(h_all[layer], du_all, ROW_CONTRACT, preferred_element_type=jnp.float32)
        if layer < layers - 1:
            g_down, g_up, grads_down[layer + 1], grads_up[layer + 1] = lax.optimization_barrier(
                (g_down, g_up, grads_down[layer + 1], grads_up[layer + 1]))
        grads_down[layer], grads_up[layer] = lax.psum((g_down, g_up), "dp")
    return jnp.stack(grads_up), jnp.stack(grads_down)


def solution(mesh):
    n_dp = mesh.shape["dp"]

    def grad_step(hidden_in, targets, w_up, w_down):
        step_fn = functools.partial(local_step, n_dp=n_dp)
        mapped = jax.shard_map(step_fn, mesh=mesh, in_specs=(P("dp", None), P("dp", None), P(None, None, "tp"), P(None, "tp", None)), out_specs=(P(None, None, "tp"), P(None, "tp", None)), check_vma=False)
        return mapped(hidden_in, targets, w_up, w_down)

    return grad_step
```

time: 1760 us -> 867 us (0.49)
  blocking collectives: 747 us -> 0 us
  waiting for transfers between devices: 828 us -> 416 us
  Pallas kernels: 0 us -> 348 us
  matrix products: 102 us -> 25.8 us
  other arithmetic: 47.7 us -> 14.3 us
  local copies, waits for them, and re-layouts: 15.5 us -> 45.8 us
    psum x4 -> x0, blocking collectives: 747 us -> none  [local_step(): branch = lax.psum(part_out, 'tp').astype(jnp.bfloat16)]
    psum x4, waiting for transfers between devices: 828 us -> 167 us  [local_step(): grads_down[layer], grads_up[layer] = lax.psum((g_down, g_up), 'dp')]
    pallas_call x0 -> x8, Pallas kernels: none -> 348 us  [the longest x4 179 us: forward_block(): pl.pallas_call(functools.partial(forward_kernel, targets is not None, gat...]
    all_gather x0 -> x12, waiting for transfers between devices: none -> 249 us  [the longest x4 116 us: gather_weights(): lax.all_gather(up, 'dp', axis=0, tiled=True)]
    dot_general x22 -> x8, matrix products: 102 us -> 25.8 us  [the longest x4 15.3 us: local_step(): lax.dot_general(act_all, g_all, ROW_CONTRACT, preferred_element_type=jnp....]
    convert_element_type x3 -> x0, other arithmetic: 19.8 us -> none  [the longest x2 12.1 us: local_step(): (g_cur.astype(jnp.float32) + lax.psum(back_part, 'tp')).astype(jnp.bfloat16)]
  transfers between devices with their start and end apart: 4 -> 16, of which waited for: 4 -> 13; matrix products, arithmetic and copies ran while one was open for 1% -> 5% of each run, Pallas kernels for 0% -> 30%
where the time goes in v1:
time: 867 us; the launch traced here: 866 us
  waiting for transfers between devices  416 us (48%)
  Pallas kernels  348 us (40%)
  local copies, waits for them, and re-layouts  45.8 us (5%)
  matrix products  25.8 us (3%)
  other arithmetic  14.3 us (2%)
  between operations  14.3 us (2%)
    pallas_call x4, Pallas kernels, forward_block(): pl.pallas_call(functools.partial(forward_kernel, targets is not None, gat...  179 us
    pallas_call x4, Pallas kernels, backward_block(): pl.pallas_call(functools.partial(backward_kernel, has_sum), out_shape=out...  170 us
    psum x4, waiting for transfers between devices, local_step(): grads_down[layer], grads_up[layer] = lax.psum((g_down, g_up), 'dp')  167 us
    all_gather x4, waiting for transfers between devices, gather_weights(): lax.all_gather(up, 'dp', axis=0, tiled=True)  116 us
    all_gather x4, waiting for transfers between devices, gather_weights(): lax.all_gather(jnp.stack([up_piece, down_piece]), 'tp', axis_index_groups...  99.4 us
    all_gather x4, waiting for transfers between devices, gather_weights(): lax.all_gather(down, 'dp', axis=0)  33.8 us
    unnamed x47, local copies, waits for them, and re-layouts  20.8 us
  transfers between devices with their start and end apart: 16, of which 13 were waited for; matrix products, arithmetic and copies ran while one was open for 5% of the time, Pallas kernels for 30%

profile of v1, /device:TPU:1, one launch (start us, length us, event | category | flops | bytes accessed | tf_op | source)
XLA Modules:
  0.0 865.7 jit_solution(14721630048161685439)
XLA Ops:
  7.2 3.9 fusion
  11.1 1.8 fusion.1
  13.0 1.0 constant_dynamic-slice_fusion.7
  14.7 1.0 constant_dynamic-slice_fusion.5
  16.5 0.9 constant_dynamic-slice_fusion.3
  19.1 23.8 %all-gather.33.cloned.1.call-done = bf16[8,256,256]{2,1,0:T(8,128)(2,1)} async-done(((bf16[2,256,256]{2,1,0:T(8,128)(2,1)}), bf16[8,256,256]{2,1,0:T(8,128)(2,1)}) %all-gather.33.cloned.1.call-update) | async-done | bytes 1048592 | tf_op jit(solution)/shard_map/all_gather | solution.py:370
  42.9 2.1 fusion.5
  46.4 25.3 %all-gather.35.cloned.1.call-done = bf16[8,256,256]{2,1,0:T(8,128)(2,1)} async-done(((bf16[2,256,256]{2,1,0:T(8,128)(2,1)}), bf16[8,256,256]{2,1,0:T(8,128)(2,1)}) %all-gather.35.cloned.1.call-update) | async-done | bytes 1048592 | tf_op jit(solution)/shard_map/all_gather | solution.py:370
  71.7 2.1 fusion.4
  75.2 25.3 %all-gather.37.cloned.1.call-done = bf16[8,256,256]{2,1,0:T(8,128)(2,1)} async-done(((bf16[2,256,256]{2,1,0:T(8,128)(2,1)}), bf16[8,256,256]{2,1,0:T(8,128)(2,1)}) %all-gather.37.cloned.1.call-update) | async-done | bytes 1048592 | tf_op jit(solution)/shard_map/all_gather | solution.py:370
  100.5 2.1 fusion.3
  104.0 25.1 %all-gather.39.cloned.1.call-done = bf16[8,256,256]{2,1,0:T(8,128)(2,1)} async-done(((bf16[2,256,256]{2,1,0:T(8,128)(2,1)}), bf16[8,256,256]{2,1,0:T(8,128)(2,1)}) %all-gather.39.cloned.1.call-update) | async-done | bytes 1048592 | tf_op jit(solution)/shard_map/all_gather | solution.py:370
  129.1 2.1 fusion.2
  132.2 1.3 constant_dynamic-slice_fusion.9.refs_0_
  135.1 33.8 %all-gather.19.cloned.1.call-done.refs_2_.refs_1_ = bf16[8,1024,256]{2,1,0:T(8,128)(2,1)} async-done(((bf16[1,1024,256]{2,1,0:T(8,128)(2,1)}), bf16[8,1024,256]{2,1,0:T(8,128)(2,1)}) %all-gather.19.cloned.1.call-update) | async-done | bytes 4194320 | tf_op jit(solution)/shard_map/all_gather | solution.py:374
  168.9 36.6 %all-gather.17.cloned.1.call-done.refs_1_ = bf16[2048,1024]{1,0:T(8,128)(2,1)} async-done(((bf16[256,1024]{1,0:T(8,128)(2,1)}), bf16[2048,1024]{1,0:T(8,128)(2,1)}) %all-gather.17.cloned.1.call-update) | async-done | bytes 4194320 | tf_op jit(solution)/shard_map/all_gather | solution.py:374
  205.5 44.2 %fwd.4 = (bf16[256,2048]{1,0:T(8,128)(2,1)S(1)}, bf16[256,1024]{1,0:T(8,128)(2,1)S(1)}, bf16[1024,256]{1,0:T(8,128)(2,1)S(1)}) custom-call(bf16[256,2048]{1,0:T(8,128)(2,1)S(1)} %constant_dynamic-slice_fusion.9.refs_0_, bf16[2048,1024]{1,0:T(8,128)(2,1)} %all-gather.17.cloned.1.call-done.refs_1_, ...), custom_call_target="tpu_custom_call" | custom-call | flops 40000000000 | bytes 20000000 | tf_op jit(solution)/shard_map/fwd/pallas_call | solution.py:334
  250.6 27.4 %all-gather.21.cloned.1.call-done.refs_1_.refs_3_ = bf16[2048,1024]{1,0:T(8,128)(2,1)} async-done(((bf16[256,1024]{1,0:T(8,128)(2,1)}), bf16[2048,1024]{1,0:T(8,128)(2,1)}) %all-gather.21.cloned.1.call-update) | async-done | bytes 4194320 | tf_op jit(solution)/shard_map/all_gather | solution.py:374
  277.9 44.7 %fwd.5 = (bf16[256,2048]{1,0:T(8,128)(2,1)S(1)}, bf16[256,1024]{1,0:T(8,128)(2,1)S(1)}, bf16[1024,256]{1,0:T(8,128)(2,1)S(1)}, bf16[1024,2048]{1,0:T(8,128)(2,1)}) custom-call(bf16[256,2048]{1,0:T(8,128)(2,1)S(1)} %get-tuple-element.41.refs_0_, bf16[2048,1024]{1,0:T(8,128)(2,1)} %all-gather.21.cloned.1.call-done.refs_1_.refs_3_, ...), custom_call_target="tpu_custom_call" | custom-call | flops 40000000000 | bytes 20000000 | tf_op jit(solution)/shard_map/fwd/pallas_call | solution.py:334
  322.7 1.0 copy-done.4
  323.6 26.6 %all-gather.25.cloned.1.call-done.refs_1_.refs_3_ = bf16[2048,1024]{1,0:T(8,128)(2,1)} async-done(((bf16[256,1024]{1,0:T(8,128)(2,1)}), bf16[2048,1024]{1,0:T(8,128)(2,1)}) %all-gather.25.cloned.1.call-update) | async-done | bytes 4194320 | tf_op jit(solution)/shard_map/all_gather | solution.py:374
  350.2 1.2 copy-done.5
  351.4 44.6 %fwd.6 = (bf16[256,2048]{1,0:T(8,128)(2,1)S(1)}, bf16[256,1024]{1,0:T(8,128)(2,1)S(1)}, bf16[1024,256]{1,0:T(8,128)(2,1)S(1)}, bf16[1024,2048]{1,0:T(8,128)(2,1)}) custom-call(bf16[256,2048]{1,0:T(8,128)(2,1)S(1)} %copy-done.5, bf16[2048,1024]{1,0:T(8,128)(2,1)} %all-gather.25.cloned.1.call-done.refs_1_.refs_3_, ...), custom_call_target="tpu_custom_call" | custom-call | flops 40000000000 | bytes 20000000 | tf_op jit(solution)/shard_map/fwd/pallas_call | solution.py:334
  396.9 25.6 %all-gather.29.cloned.1.call-done.refs_1_.refs_3_ = bf16[2048,1024]{1,0:T(8,128)(2,1)} async-done(((bf16[256,1024]{1,0:T(8,128)(2,1)}), bf16[2048,1024]{1,0:T(8,128)(2,1)}) %all-gather.29.cloned.1.call-update) | async-done | bytes 4194320 | tf_op jit(solution)/shard_map/all_gather | solution.py:374
  422.5 44.9 %fwd.7 = (bf16[256,2048]{1,0:T(8,128)(2,1)S(1)}, bf16[256,1024]{1,0:T(8,128)(2,1)S(1)}, bf16[1024,256]{1,0:T(8,128)(2,1)S(1)}, bf16[1024,2048]{1,0:T(8,128)(2,1)}) custom-call(bf16[256,2048]{1,0:T(8,128)(2,1)S(1)} %get-tuple-element.43.refs_0_, bf16[2048,1024]{1,0:T(8,128)(2,1)} %all-gather.29.cloned.1.call-done.refs_1_.refs_3_, ...), custom_call_target="tpu_custom_call" | custom-call | flops 40000000000 | bytes 20000000 | tf_op jit(solution)/shard_map/fwd/pallas_call | solution.py:334
  467.5 42.7 %bwd.4 = (bf16[256,2048]{1,0:T(8,128)(2,1)S(1)}, bf16[1024,256]{1,0:T(8,128)(2,1)S(1)}, bf16[1024,2048]{1,0:T(8,128)(2,1)}) custom-call(bf16[256,2048]{1,0:T(8,128)(2,1)S(1)} %get-tuple-element.44.refs_0_, bf16[8,1024,256]{2,1,0:T(8,128)(2,1)} %all-gather.31.cloned.1.call-done.refs_2_.refs_1_, bf16[256,1024]{1,0:T(8,128)(2,1)S(1)} %get-tuple-element.45.refs_2_, ...), custom_call_target="tpu_custom_call" | custom-call | flops 40000000000 | bytes 20000000 | tf_op jit(solution)/shard_map/bwd/pallas_call | solution.py:360
  510.2 2.6 fusion.12
  513.5 2.6 fusion.11
  516.4 1.2 copy-done.3
  517.6 1.0 copy-done.7
  518.7 41.5 %bwd.5 = (bf16[256,2048]{1,0:T(8,128)(2,1)S(1)}, bf16[1024,256]{1,0:T(8,128)(2,1)S(1)}, bf16[1024,2048]{1,0:T(8,128)(2,1)}) custom-call(bf16[256,2048]{1,0:T(8,128)(2,1)S(1)} %copy-done.3, bf16[8,1024,256]{2,1,0:T(8,128)(2,1)} %all-gather.27.cloned.1.call-done.refs_2_.refs_1_, bf16[256,1024]{1,0:T(8,128)(2,1)S(1)} %copy-done.7, ...), custom_call_target="tpu_custom_call" | custom-call | flops 40000000000 | bytes 20000000 | tf_op jit(solution)/shard_map/bwd/pallas_call | solution.py:360
  560.2 4.9 fusion.9
  565.1 2.6 fusion.10
  567.7 28.9 %all-reduce.15.cloned.1.call-done = (f32[256,2048]{1,0:T(8,128)}, f32[2048,256]{0,1:T(8,128)}) async-done(((f32[256,2048]{1,0:T(8,128)}, f32[2048,256]{0,1:T(8,128)}), (f32[256,2048]{1,0:T(8,128)}, f32[2048,256]{0,1:T(8,128)})) %all-reduce.15.cloned.1.call-update) | async-done | bytes 4194320 | tf_op jit(solution)/shard_map/psum | solution.py:412
  596.6 2.9 copy.23
  599.6 43.9 %bwd.6 = (bf16[256,2048]{1,0:T(8,128)(2,1)S(1)}, bf16[1024,256]{1,0:T(8,128)(2,1)S(1)}, bf16[1024,2048]{1,0:T(8,128)(2,1)}) custom-call(bf16[256,2048]{1,0:T(8,128)(2,1)S(1)} %get-tuple-element.48.refs_0_, bf16[8,1024,256]{2,1,0:T(8,128)(2,1)} %all-gather.23.cloned.1.call-done.refs_2_.refs_1_, bf16[256,1024]{1,0:T(8,128)(2,1)S(1)} %get-tuple-element.49.refs_2_, ...), custom_call_target="tpu_custom_call" | custom-call | flops 40000000000 | bytes 20000000 | tf_op jit(solution)/shard_map/bwd/pallas_call | solution.py:360
  643.5 5.2 fusion.7
  648.7 2.6 fusion.8
  651.4 26.5 %all-reduce.13.cloned.1.call-done = (f32[256,2048]{1,0:T(8,128)}, f32[2048,256]{0,1:T(8,128)}) async-done(((f32[256,2048]{1,0:T(8,128)}, f32[2048,256]{0,1:T(8,128)}), (f32[256,2048]{1,0:T(8,128)}, f32[2048,256]{0,1:T(8,128)})) %all-reduce.13.cloned.1.call-update) | async-done | bytes 4194320 | tf_op jit(solution)/shard_map/psum | solution.py:412
  677.8 3.0 copy.24
  680.9 41.5 %bwd.7 = (bf16[1024,256]{1,0:T(8,128)(2,1)S(1)}, bf16[1024,2048]{1,0:T(8,128)(2,1)}) custom-call(bf16[256,2048]{1,0:T(8,128)(2,1)S(1)} %copy-done.1, bf16[8,1024,256]{2,1,0:T(8,128)(2,1)} %all-gather.19.cloned.1.call-done.refs_2_.refs_1_, bf16[256,1024]{1,0:T(8,128)(2,1)S(1)} %copy-done.9), custom_call_target="tpu_custom_call" | custom-call | flops 40000000000 | bytes 20000000 | tf_op jit(solution)/shard_map/bwd/pallas_call | solution.py:360
  722.5 2.6 convolution_bitcast_fusion
  725.1 2.6 fusion.6
  727.7 31.6 %all-reduce.11.cloned.1.call-done = (f32[256,2048]{1,0:T(8,128)}, f32[2048,256]{0,1:T(8,128)}) async-done(((f32[256,2048]{1,0:T(8,128)}, f32[2048,256]{0,1:T(8,128)}), (f32[256,2048]{1,0:T(8,128)}, f32[2048,256]{0,1:T(8,128)})) %all-reduce.11.cloned.1.call-update) | async-done | bytes 4194320 | tf_op jit(solution)/shard_map/psum | solution.py:412
  759.3 79.7 %all-reduce.9.cloned.1.call-done = (f32[1,2048,256]{1,2,0:T(8,128)}, f32[1,256,2048]{2,1,0:T(8,128)}) async-done(((f32[1,2048,256]{1,2,0:T(8,128)}, f32[1,256,2048]{2,1,0:T(8,128)}), (f32[1,2048,256]{1,2,0:T(8,128)}, f32[1,256,2048]{2,1,0:T(8,128)})) %all-reduce.9.cloned.1.call-update) | async-done | bytes 4194320 | tf_op jit(solution)/shard_map/psum | solution.py:412
  839.0 5.7 pad_maximum_fusion
  844.7 8.8 %copy.25 = f32[4,2048,256]{2,1,0:T(8,128)} copy(f32[4,2048,256]{1,2,0:T(8,128)} %pad_maximum_fusion) | data formatting | bytes 16777216
  853.5 5.7 pad_maximum_fusion.1
  (83 shorter events, 12.8 us)
Async XLA Ops:
  7.2 35.7 %all-gather.33.cloned.1.call-start = ((), (), s32[]{:S(2)}) async-start(), calls=%async_computation.8 | async-start | bytes 1310720 | tf_op jit(solution)/shard_map/all_gather | solution.py:370
  7.2 3.9 copy-start.10
  14.7 57.0 %all-gather.35.cloned.1.call-start = ((), (), s32[]{:S(2)}) async-start(), calls=%async_computation.9 | async-start | bytes 1310720 | tf_op jit(solution)/shard_map/all_gather | solution.py:370
  16.5 84.0 %all-gather.37.cloned.1.call-start = ((), (), s32[]{:S(2)}) async-start(), calls=%async_computation.10 | async-start | bytes 1310720 | tf_op jit(solution)/shard_map/all_gather | solution.py:370
  18.2 110.9 %all-gather.39.cloned.1.call-start = ((), (), s32[]{:S(2)}) async-start(), calls=%async_computation.11 | async-start | bytes 1310720 | tf_op jit(solution)/shard_map/all_gather | solution.py:370
  19.1 149.8 %all-gather.19.cloned.1.call-start = ((), (), s32[]{:S(2)}) async-start(), calls=%async_computation.1 | async-start | bytes 4718592 | tf_op jit(solution)/shard_map/all_gather | solution.py:374
  45.0 160.5 %all-gather.17.cloned.1.call-start = ((), (), s32[]{:S(2)}) async-start(), calls=%async_computation | async-start | bytes 4718592 | tf_op jit(solution)/shard_map/all_gather | solution.py:374
  46.4 204.2 %all-gather.23.cloned.1.call-start = ((), (), s32[]{:S(2)}) async-start(), calls=%async_computation.3 | async-start | bytes 4718592 | tf_op jit(solution)/shard_map/all_gather | solution.py:374
  73.8 204.2 %all-gather.21.cloned.1.call-start = ((), (), s32[]{:S(2)}) async-start(), calls=%async_computation.2 | async-start | bytes 4718592 | tf_op jit(solution)/shard_map/all_gather | solution.py:374
  75.2 248.5 %all-gather.27.cloned.1.call-start = ((), (), s32[]{:S(2)}) async-start(), calls=%async_computation.5 | async-start | bytes 4718592 | tf_op jit(solution)/shard_map/all_gather | solution.py:374
  102.6 247.6 %all-gather.25.cloned.1.call-start = ((), (), s32[]{:S(2)}) async-start(), calls=%async_computation.4 | async-start | bytes 4718592 | tf_op jit(solution)/shard_map/all_gather | solution.py:374
  104.0 292.9 %all-gather.31.cloned.1.call-start = ((), (), s32[]{:S(2)}) async-start(), calls=%async_computation.7 | async-start | bytes 4718592 | tf_op jit(solution)/shard_map/all_gather | solution.py:374
  131.2 291.3 %all-gather.29.cloned.1.call-start = ((), (), s32[]{:S(2)}) async-start(), calls=%async_computation.6 | async-start | bytes 4718592 | tf_op jit(solution)/shard_map/all_gather | solution.py:374
  134.8 461.8 %all-reduce.15.cloned.1.call-start = ((), (), s32[]{:S(2)}) async-start(), calls=%async_computation.15 | async-start | bytes 8388608 | tf_op jit(solution)/shard_map/psum | solution.py:412
  249.8 0.8 copy-start.8
  322.7 1.0 copy-start.4
  350.2 1.2 copy-start.5
  396.1 0.8 copy-start.6
  467.5 42.7 %copy-start.14 = (bf16[1024,2048]{1,0:T(8,128)(2,1)S(1)}, bf16[1024,2048]{1,0:T(8,128)(2,1)}, u32[]{:S(2)}) copy-start(bf16[1024,2048]{1,0:T(8,128)(2,1)} %get-tuple-element.64) | copy-start | bytes 12582916
  510.2 2.6 copy-start.2
  510.2 3.3 copy-start.15
  516.1 161.7 %all-reduce.13.cloned.1.call-start = ((), (), s32[]{:S(2)}) async-start(), calls=%async_computation.14 | async-start | bytes 8388608 | tf_op jit(solution)/shard_map/psum | solution.py:412
  516.4 1.2 copy-start.3
  517.6 1.0 copy-start.7
  560.1 4.9 copy-start.18
  599.5 159.8 %all-reduce.11.cloned.1.call-start = ((), (), s32[]{:S(2)}) async-start(), calls=%async_computation.13 | async-start | bytes 8388608 | tf_op jit(solution)/shard_map/psum | solution.py:412
  643.5 5.2 copy-start
  643.5 5.2 copy-start.17
  677.8 3.1 copy-start.1
  677.8 3.1 copy-start.9
  680.8 158.1 %all-reduce.9.cloned.1.call-start = ((), (), s32[]{:S(2)}) async-start(), calls=%async_computation.12 | async-start | bytes 8388608 | tf_op jit(solution)/shard_map/psum | solution.py:412
  680.9 41.6 %copy-start.13 = (bf16[1024,2048]{1,0:T(8,128)(2,1)S(1)}, bf16[1024,2048]{1,0:T(8,128)(2,1)}, u32[]{:S(2)}) copy-start(bf16[1024,2048]{1,0:T(8,128)(2,1)} %param.4) | copy-start | bytes 12582916
  722.5 2.6 copy-start.16
  725.1 113.9 %copy-start.12 = (f32[2048,256]{0,1:T(8,128)S(1)}, f32[2048,256]{0,1:T(8,128)}, u32[]{:S(2)}) copy-start(f32[2048,256]{0,1:T(8,128)} %get-tuple-element.73) | copy-start | bytes 6291460
  844.7 8.8 %copy-start.11 = (f32[256,2048]{1,0:T(8,128)S(1)}, f32[256,2048]{1,0:T(8,128)}, u32[]{:S(2)}) copy-start(f32[256,2048]{1,0:T(8,128)} %get-tuple-element.77) | copy-start | bytes 6291460
Sparse Core Ops, SparseCore 0:
  14.8 28.0 all-gather.32
  44.7 26.9 all-gather.34
  73.5 26.9 all-gather.36
  102.1 26.9 all-gather.38
  131.4 37.4 all-gather.18
  171.2 34.3 all-gather.16
  207.4 34.3 all-gather.22
  243.6 34.3 all-gather.20
  279.8 34.3 all-gather.26
  315.9 34.3 all-gather.24
  352.1 34.3 all-gather.30
  388.2 34.3 all-gather.28
  516.2 80.3 all-reduce.14
  599.6 78.1 all-reduce.12
  681.0 78.2 all-reduce.10
  761.6 77.3 all-reduce.8

commit v2 on v0

v2 whole, which is shorter than its diff:
```python
import functools
import jax
import jax.numpy as jnp
from jax import lax
from jax.experimental import pallas as pl
from jax.experimental.pallas import tpu as pltpu
from jax.sharding import PartitionSpec as P

NZ, NY, NX = 8, 4, 4
COPIES, LOCALS = 96, 32
ROW_CONTRACT = (((0,), (0,)), ((), ()))
COL_CONTRACT = (((1,), (1,)), ((), ()))
Z_CHAINS = ((0, 0, 4), (1, 0, 3), (1, 1, 4), (0, 1, 3))
X_CHAINS = ((0, 0, 2), (1, 0, 1), (1, 1, 2), (0, 1, 1))
ANY = pl.BlockSpec(memory_space=pl.ANY)
VMEM = pl.BlockSpec(memory_space=pltpu.VMEM)
BF16, F32 = jnp.bfloat16, jnp.float32


def gelu_tanh(value):
    return jax.nn.gelu(value, approximate=True)


def at(start, size):
    return pl.ds(pl.multiple_of(start, size), size)


def shift(position, amount, size):
    return lax.rem(position + amount % size, size)


class Net:
    def __init__(self, send_sem, recv_sem, local_sem):
        tp, dp = lax.axis_index("tp"), lax.axis_index("dp")
        self.z, self.y = lax.div(tp, NY), lax.rem(tp, NY)
        self.x, self.c = lax.div(dp, 2), lax.rem(dp, 2)
        self.send_sem, self.recv_sem, self.local_sem = send_sem, recv_sem, local_sem
        self.n_copies = self.n_locals = 0

    def device(self, dz=0, dy=0, dx=0, other_core=False):
        z, y, x = shift(self.z, dz, NZ), shift(self.y, dy, NY), shift(self.x, dx, NX)
        c = 1 - self.c if other_core else self.c
        return {"tp": z * NY + y, "dp": x * 2 + c}

    def barrier(self, **axes):
        peers = []
        if axes.get("y"):
            peers += [self.device(dy=s) for s in (1, 2, 3)]
        if axes.get("z"):
            peers += [self.device(dz=s) for s in (1, -1)]
        if axes.get("x"):
            peers += [self.device(dx=s) for s in (1, -1)] + [self.device(other_core=True)]
        sem = pltpu.get_barrier_semaphore()
        for peer in peers:
            pl.semaphore_signal(sem, inc=1, device_id=peer, device_id_type=pl.DeviceIdType.MESH)
        pl.semaphore_wait(sem, len(peers))

    def copy(self, src, dst, **where):
        index = self.n_copies
        self.n_copies += 1
        return pltpu.make_async_remote_copy(
            src_ref=src, dst_ref=dst, send_sem=self.send_sem.at[index], recv_sem=self.recv_sem.at[index],
            device_id=self.device(**where), device_id_type=pl.DeviceIdType.MESH)

    def local(self, src, dst):
        index = self.n_locals
        self.n_locals += 1
        return pltpu.make_async_copy(src, dst, self.local_sem.at[index])


class RowGather:
    def __init__(self, net, block, out):
        rows = block.shape[0]
        half = rows // 2
        below, above = shift(net.y, -1, NY), shift(net.y, 1, NY)
        own = out.at[at(net.y * rows, rows)]
        lower, upper = out.at[at(below * rows, half)], out.at[at(above * rows + half, half)]
        self.local = net.local(block, own)
        self.first = [net.copy(block, own, dy=1), net.copy(block, own, dy=-1)]
        self.second = [net.copy(lower, lower, dy=1), net.copy(upper, upper, dy=-1)]

    def start(self):
        self.local.start()
        for copy in self.first:
            copy.start()

    def relay(self):
        for copy, onward in zip(self.first, self.second):
            copy.wait_recv()
            onward.start()

    def finish(self):
        self.local.wait()
        for copy in self.first:
            copy.wait_send()
        for copy in self.second:
            copy.wait()


class ColumnExchange:
    def __init__(self, net, block, out):
        rows, cols = block.shape[0], block.shape[1] // NY
        own = out.at[at(net.y * rows, rows)]
        self.local = net.local(block.at[:, 0:cols], own)
        self.copies = [net.copy(block.at[:, s * cols:(s + 1) * cols], own, dy=s) for s in (1, 3, 2)]

    def start(self):
        self.local.start()
        for copy in self.copies:
            copy.start()

    def finish(self):
        self.local.wait()
        for copy in self.copies:
            copy.wait()


class PieceFetch:
    def __init__(self, net, w_up, w_down, up, down):
        piece = up.shape[1]
        cols = w_down.shape[0]
        dp = net.x * 2 + net.c
        up_piece, down_piece = w_up.at[at(dp * piece, piece)], w_down.at[:, at(dp * piece, piece)]
        self.copies = []
        for s in (1, 3, 2):
            slot = NY - s - 1
            self.copies.append(net.copy(up_piece, up.at[slot], dy=s))
            self.copies.append(net.copy(down_piece, down.at[slot * cols:(slot + 1) * cols], dy=s))

    def start(self):
        for copy in self.copies:
            copy.start()

    def finish(self):
        for copy in self.copies:
            copy.wait()


class PieceSpread:
    def __init__(self, net, up, down, all_up, all_down):
        piece, tall = up.shape[1], down.shape[0]

        def views(dx, half=None):
            dp = shift(net.x, dx, NX) * 2 + net.c
            if half is None:
                return all_up.at[:, at(dp * piece, piece)], all_down.at[dp]
            return (all_up.at[:, at(dp * piece + half * (piece // 2), piece // 2)],
                    all_down.at[dp, half * (tall // 2):(half + 1) * (tall // 2)])

        own = views(0)
        self.local = [net.local(a, b) for a, b in zip((up, down), own)]
        self.first = [[net.copy(a, b, dx=d) for a, b in zip((up, down), own)] for d in (1, -1)]
        self.second = [[net.copy(v, v, dx=d) for v in views(-d, half)] for half, d in ((0, 1), (1, -1))]
        self.across = [[net.copy(a, b, other_core=True) for a, b in zip((up, down), own)]]
        self.across += [[net.copy(v, v, other_core=True) for v in views(d)] for d in (-1, 1, 2)]

    def start(self):
        for copies in (self.local, *self.first, self.across[0]):
            for copy in copies:
                copy.start()

    def relay(self):
        for first, second, across in zip(self.first, self.second, self.across[1:3]):
            for copy in first:
                copy.wait_recv()
            for copy in (*second, *across):
                copy.start()

    def cross(self):
        for copies in self.second:
            for copy in copies:
                copy.wait_recv()
        for copy in self.across[3]:
            copy.start()

    def finish(self):
        for copy in self.local:
            copy.wait()
        for copies in (*self.first, *self.second):
            for copy in copies:
                copy.wait_send()
        for copies in self.across:
            for copy in copies:
                copy.wait()


class Ring:
    def __init__(self, net, axis, chains, part, slot, out):
        self.net, self.axis, self.chains = net, axis, chains
        self.size = {"x": NX, "z": NZ}[axis]
        self.here = {"x": net.x, "z": net.z}[axis]
        self.part, self.slot, self.out = part, slot, out
        self.copies, self.last = [], {}

    def owner(self, direction, amount):
        return shift(self.here, amount if direction == 0 else -amount, self.size)

    def send(self, chain, src, dst):
        direction = self.chains[chain][0]
        copy = self.net.copy(src, dst, **{"d" + self.axis: 1 if direction == 0 else -1})
        copy.start()
        self.copies.append(copy)
        self.last[chain] = copy

    def reduce(self, chain, step):
        direction, half, hops = self.chains[chain]
        if step >= hops:
            return
        mine = self.part(self.owner(direction, hops - step), half)
        if step > 0:
            self.last[chain].wait_recv()
            mine[...] = mine[...] + self.slot(chain, step - 1)[...]
        self.send(chain, mine, self.slot(chain, step))

    def reduce_half(self, half):
        for chain, (_, h, _) in enumerate(self.chains):
            if h == half:
                self.reduce(chain, 0)

    def reduce_all(self, step):
        for chain in range(len(self.chains)):
            self.reduce(chain, step)

    def total(self, half):
        value = self.part(self.here, half)[...]
        for chain, (_, h, hops) in enumerate(self.chains):
            if h == half:
                self.last[chain].wait_recv()
                value = value + self.slot(chain, hops - 1)[...]
        return value

    def gather(self, chain, step, first=None):
        direction, half, hops = self.chains[chain]
        if step >= hops:
            return
        if step > 0:
            self.last[chain].wait_recv()
        held = self.out(self.owner(direction, -step), half)
        self.send(chain, held if first is None else first, held)

    def gather_all(self, step):
        for chain in range(len(self.chains)):
            self.gather(chain, step)

    def arrived(self):
        for copy in self.last.values():
            copy.wait_recv()

    def finish(self):
        for copy in self.copies:
            copy.wait_send()


def slot_index(chains, chain, step):
    return sum(hops for _, _, hops in chains[:chain]) + step


def z_ring(net, part, slots, out):
    rows, cols = part.shape[0] // NZ, part.shape[1] // 2

    def block(ref):
        return lambda owner, half: ref.at[at(owner * rows, rows), half * cols:(half + 1) * cols]

    ring = Ring(net, "z", Z_CHAINS, block(part), lambda chain, step: slots.at[slot_index(Z_CHAINS, chain, step)], block(out))
    ring.block = block
    return ring


class GradSum:
    def __init__(self, net, act, g_all, h_all, d_pre, out_up, out_down, scratch):
        (self.act, self.g, self.h, self.d, self.up, self.down, self.sib_up, self.sib_down, slots_up, slots_down) = scratch
        self.net, self.outs = net, (out_up, out_down)
        self.loads = [net.local(a, b) for a, b in zip((act, g_all, h_all, d_pre), (self.act, self.g, self.h, self.d))]
        parts, slots = (self.up, self.down), (slots_up, slots_down)

        def slot(chain, step):
            half = X_CHAINS[chain][1]
            before = sum(hops for _, h, hops in X_CHAINS[:chain] if h == half)
            return slots[half].at[before + step]

        self.ring = Ring(net, "x", X_CHAINS, lambda owner, half: parts[half].at[owner, net.c], slot,
                         lambda owner, half: self.outs[half].at[owner, net.c])
        other = 1 - net.c
        self.swap = [net.copy(self.up.at[:, other], self.sib_up, other_core=True),
                     net.copy(self.down.at[:, other], self.sib_down, other_core=True)]
        self.across, self.local = [], []

    def load(self):
        for copy in self.loads:
            copy.start()

    def products(self):
        for copy in self.loads:
            copy.wait()
        tall, wide = self.up.shape[2], self.up.shape[3]
        rows = self.down.shape[2]

        @pl.loop(0, 2 * NX)
        def _(n):
            cols = at(n * tall, tall)
            self.up[lax.div(n, 2), lax.rem(n, 2)] = lax.dot_general(self.h[:, cols], self.d[...], ROW_CONTRACT, preferred_element_type=F32)

        self.swap[0].start()

        @pl.loop(0, 2 * NX)
        def _(n):
            cols = at(n * tall, tall)
            tile = lax.dot_general(self.act[...], self.g[:, cols], ROW_CONTRACT, preferred_element_type=F32)
            self.down[:, :, :, cols] = tile.reshape(NX, 2, rows, tall)

        self.swap[1].start()

    def merge(self):
        c = self.net.c
        for half, (mine, other) in enumerate(((self.up, self.sib_up), (self.down, self.sib_down))):
            self.swap[half].wait_recv()
            for k in range(NX):
                mine[k, c] = mine[k, c] + other[k]
            self.ring.reduce_half(half)

    def cross(self, src, dst):
        copy = self.net.copy(src, dst, other_core=True)
        copy.start()
        self.across.append(copy)

    def settle(self):
        x, c = self.net.x, self.net.c
        for half, mine in enumerate((self.up, self.down)):
            own = mine.at[x, c]
            own[...] = self.ring.total(half)
            out = self.outs[half].at[x, c]
            for chain, (_, h, _) in enumerate(X_CHAINS):
                if h == half:
                    self.ring.gather(chain, 0, own)
            copy = self.net.local(own, out)
            copy.start()
            self.local.append(copy)
            self.cross(own, out)

    def finish(self):
        self.ring.gather_all(1)
        for half in (0, 1):
            for dx in (1, -1):
                out = self.outs[half].at[shift(self.net.x, dx, NX), self.net.c]
                if (half == 0) != (dx == 1):
                    self.cross(out, out)
        self.ring.arrived()
        for half in (0, 1):
            for dx in (1, -1):
                out = self.outs[half].at[shift(self.net.x, dx, NX), self.net.c]
                if (half == 0) == (dx == 1):
                    self.cross(out, out)
            out = self.outs[half].at[shift(self.net.x, 2, NX), self.net.c]
            self.cross(out, out)
        for copy in self.local:
            copy.wait()
        for copy in self.swap:
            copy.wait_send()
        self.ring.finish()
        for copy in self.across:
            copy.wait()


class Weights:
    def __init__(self, net, w_up, w_down, all_up, all_down, wu, wd):
        cols, blocks = w_down.shape[0], all_down.shape[0]
        piece = all_down.shape[2]
        self.up = []
        if wu is not None:
            self.up = [net.local(w_up, wu.at[:, 0:cols])]
            self.up += [net.local(all_up.at[s], wu.at[:, (s + 1) * cols:(s + 2) * cols]) for s in range(NY - 1)]
        self.down = [net.local(w_down, wd.at[0:cols])]
        self.down += [net.local(all_down.at[n], wd.at[cols:, n * piece:(n + 1) * piece]) for n in range(blocks)]

    def start(self, copies):
        for copy in copies:
            copy.start()

    def wait(self, copies):
        for copy in copies:
            copy.wait()


def take(refs, count):
    taken = refs[:count]
    del refs[:count]
    return taken if count > 1 else taken[0]


def start_kernel(*refs):
    refs = list(refs)
    w_up, w_down, all_up, all_down, next_up, next_down, up, down = take(refs, 8)
    net = Net(*refs)
    net.barrier(y=True, x=True)
    fetch = PieceFetch(net, w_up.at[0], w_down.at[0], up, down)
    ahead = PieceFetch(net, w_up.at[1], w_down.at[1], next_up, next_down)
    spread = PieceSpread(net, up, down, all_up, all_down)
    fetch.start()
    fetch.finish()
    spread.start()
    ahead.start()
    spread.relay()
    spread.cross()
    spread.finish()
    ahead.finish()


def forward_kernel(layer, layers, total_tokens, *refs):
    refs = list(refs)
    is_last, gather_h, spreads, fetches = layer == layers - 1, layer > 0, layer + 1 < layers, layer + 2 < layers
    h_ref, w_up, w_down, all_up, all_down = take(refs, 5)
    t_ref = take(refs, 1) if is_last else None
    held = take(refs, 2) if spreads else None
    out_ref, u_ref, a_out = take(refs, 3)
    h_out = take(refs, 1) if gather_h else None
    nexts = take(refs, 2) if spreads else None
    fetched = take(refs, 2) if fetches else None
    wu, wd, act, part, slots = take(refs, 5)
    net = Net(*refs)
    weights = Weights(net, w_up.at[layer], w_down.at[layer], all_up, all_down, wu, wd)
    weights.start(weights.up)
    weights.start(weights.down)
    net.barrier(y=True, z=True, x=spreads)
    if gather_h:
        rows = RowGather(net, h_ref, h_out)
        rows.start()
    if spreads:
        spread = PieceSpread(net, *held, *nexts)
        spread.start()
    if fetches:
        fetch = PieceFetch(net, w_up.at[layer + 2], w_down.at[layer + 2], *fetched)
    cols = wu.shape[1] // NY
    weights.wait(weights.up)

    @pl.loop(0, NY)
    def _(n):
        block = at(n * cols, cols)
        pre = jnp.dot(h_ref[...], wu[:, block], preferred_element_type=F32).astype(BF16)
        u_ref[:, block] = pre
        act[:, block] = gelu_tanh(pre.astype(F32)).astype(BF16)

    ring = z_ring(net, part, slots, out_ref)
    exchange = ColumnExchange(net, act, a_out)
    tile = part.shape[1] // 8

    def down(n):
        part[:, at(n * tile, tile)] = jnp.dot(act[...], wd[:, at(n * tile, tile)], preferred_element_type=F32)

    weights.wait(weights.down)
    pl.loop(0, 4)(down)
    ring.reduce_half(0)
    pl.loop(4, 8)(down)
    ring.reduce_half(1)
    exchange.start()
    if fetches:
        fetch.start()
    for step in (1, 2, 3):
        ring.reduce_all(step)
    for half in (0, 1):
        branch = ring.total(half).astype(BF16)
        value = ring.block(h_ref)(net.z, half)[...] + branch
        if is_last:
            width = value.shape[1]
            err = value.astype(F32) - t_ref[:, half * width:(half + 1) * width].astype(F32)
            value = (err / total_tokens).astype(BF16)
        ring.out(net.z, half)[...] = value
    ring.gather_all(0)
    if spreads:
        spread.relay()
    ring.gather_all(1)
    if gather_h:
        rows.relay()
    ring.gather_all(2)
    ring.gather_all(3)
    if spreads:
        spread.cross()
    ring.arrived()
    ring.finish()
    exchange.finish()
    if fetches:
        fetch.finish()
    if gather_h:
        rows.finish()
    if spreads:
        spread.finish()


def backward_kernel(layer, layers, *refs):
    refs = list(refs)
    has_sum, has_grads = layer > 0, layer < layers - 1
    g_ref, u_ref, w_up, w_down, all_up, all_down = take(refs, 6)
    terms = take(refs, 4) if has_grads else None
    du_out, g_out = take(refs, 2)
    out_ref = take(refs, 1) if has_sum else None
    sums = take(refs, 2) if has_grads else None
    wd, dpre = take(refs, 2)
    if has_sum:
        wu, part, slots = take(refs, 3)
    scratch = take(refs, 10) if has_grads else None
    net = Net(*refs)
    weights = Weights(net, w_up.at[layer], w_down.at[layer], all_up, all_down, wu if has_sum else None, wd)
    weights.start(weights.down)
    if has_sum:
        weights.start(weights.up)
    if has_grads:
        grads = GradSum(net, *terms, *sums, scratch)
        grads.load()
    net.barrier(y=True, z=has_sum, x=has_grads)
    rows = RowGather(net, g_ref, g_out)
    rows.start()
    weights.wait(weights.down)
    cols = wd.shape[0] // NY

    @pl.loop(0, NY)
    def _(n):
        block = at(n * cols, cols)
        d_act = lax.dot_general(g_ref[...], wd[block, :], COL_CONTRACT, preferred_element_type=F32)
        _, gelu_vjp = jax.vjp(gelu_tanh, u_ref[:, block].astype(F32))
        dpre[:, block] = gelu_vjp(d_act)[0].astype(BF16)

    exchange = ColumnExchange(net, dpre, du_out)
    if not has_sum:
        exchange.start()
        grads.products()
        grads.merge()
        grads.ring.reduce_all(1)
        rows.relay()
        grads.settle()
        exchange.finish()
        rows.finish()
        grads.finish()
        return
    weights.wait(weights.up)
    ring = z_ring(net, part, slots, out_ref)
    tile = wu.shape[0] // 8

    def back(n):
        part[:, at(n * tile, tile)] = lax.dot_general(dpre[...], wu[at(n * tile, tile), :], COL_CONTRACT, preferred_element_type=F32)

    pl.loop(0, 4)(back)
    ring.reduce_half(0)
    pl.loop(4, 8)(back)
    ring.reduce_half(1)
    exchange.start()
    if has_grads:
        grads.products()
    ring.reduce_all(1)
    if has_grads:
        grads.merge()
    ring.reduce_all(2)
    ring.reduce_all(3)
    for half in (0, 1):
        total = ring.total(half)
        ring.out(net.z, half)[...] = (ring.block(g_ref)(net.z, half)[...].astype(F32) + total).astype(BF16)
    ring.gather_all(0)
    if has_grads:
        grads.ring.reduce_all(1)
    ring.gather_all(1)
    rows.relay()
    ring.gather_all(2)
    if has_grads:
        grads.settle()
    ring.gather_all(3)
    ring.arrived()
    ring.finish()
    exchange.finish()
    rows.finish()
    if has_grads:
        grads.finish()


def last_kernel(*refs):
    refs = list(refs)
    terms, sums, scratch = take(refs, 4), take(refs, 2), take(refs, 10)
    net = Net(*refs)
    grads = GradSum(net, *terms, *sums, scratch)
    grads.load()
    net.barrier(x=True)
    grads.products()
    grads.merge()
    grads.ring.reduce_all(1)
    grads.settle()
    grads.finish()


def call(kernel, name, collective_id, args, in_specs, outs, out_specs, scratch):
    sems = [pltpu.SemaphoreType.DMA((COPIES,)), pltpu.SemaphoreType.DMA((COPIES,)), pltpu.SemaphoreType.DMA((LOCALS,))]
    return pl.pallas_call(
        kernel, out_shape=outs, in_specs=in_specs, out_specs=out_specs, scratch_shapes=scratch + sems, name=name,
        compiler_params=pltpu.CompilerParams(collective_id=collective_id, has_side_effects=True, vmem_limit_bytes=60 * 1024 * 1024),
        cost_estimate=pl.CostEstimate(flops=40_000_000_000, bytes_accessed=20_000_000, transcendentals=0),
    )(*args)


class Plan:
    def __init__(self, hidden, w_up, n_dp):
        self.layers, self.width, self.cols = w_up.shape
        self.tokens = hidden.shape[0]
        self.rows = self.tokens // NY
        self.hidden = self.cols * NY
        self.n_dp = n_dp
        self.piece = self.width // n_dp

    def gathered(self):
        return [jax.ShapeDtypeStruct((NY - 1, self.width, self.cols), BF16),
                jax.ShapeDtypeStruct((self.n_dp, (NY - 1) * self.cols, self.piece), BF16)]

    def fetched(self):
        return [jax.ShapeDtypeStruct((NY - 1, self.piece, self.cols), BF16),
                jax.ShapeDtypeStruct(((NY - 1) * self.cols, self.piece), BF16)]

    def sum_scratch(self):
        return [pltpu.VMEM((self.rows, self.width), F32), pltpu.VMEM((14, self.rows // NZ, self.width // 2), F32)]

    def grad_outs(self):
        return [jax.ShapeDtypeStruct((NX, 2, self.width // 8, self.cols), F32),
                jax.ShapeDtypeStruct((NX, 2, self.cols // 8, self.width), F32)]

    def grad_scratch(self):
        up, down = self.grad_outs()
        shapes = [up.shape, down.shape, (NX, *up.shape[2:]), (NX, *down.shape[2:]), (3, *up.shape[2:]), (3, *down.shape[2:])]
        loads = [(self.tokens, self.cols), (self.tokens, self.width), (self.tokens, self.width), (self.tokens, self.cols)]
        return [pltpu.VMEM(s, BF16) for s in loads] + [pltpu.VMEM(s, F32) for s in shapes]


def struct(*shape):
    return jax.ShapeDtypeStruct(shape, BF16)


def vmem(array):
    return pltpu.VMEM(array.shape, array.dtype)


def local_step(hidden, targets, w_up, w_down, n_dp):
    plan = Plan(hidden, w_up, n_dp)
    layers, width, rows = plan.layers, plan.width, plan.rows
    tp = lax.axis_index("tp")
    z, y = lax.div(tp, NY), lax.rem(tp, NY)
    h_cur = lax.dynamic_slice(hidden, (y * rows, 0), (rows, width))
    t_own = lax.dynamic_slice(targets, (y * rows + z * (rows // NZ), 0), (rows // NZ, width))
    outs = call(start_kernel, "start", 0, [w_up, w_down], [ANY, ANY], plan.gathered() + plan.fetched(), [ANY, ANY, VMEM, VMEM],
                [vmem(a) for a in plan.fetched()])
    weights, held = [outs[:2]], outs[2:]
    wu, wd = pltpu.VMEM((width, plan.hidden), BF16), pltpu.VMEM((plan.hidden, width), BF16)
    act = pltpu.VMEM((rows, plan.hidden), BF16)
    saved, h_all = [], [hidden]
    for layer in range(layers):
        args, in_specs = [h_cur, w_up, w_down, *weights[layer]], [VMEM] + [ANY] * 4
        shapes = [struct(rows, width), struct(rows, plan.hidden), struct(plan.tokens, plan.cols)]
        out_specs = [VMEM, VMEM, ANY]
        if layer == layers - 1:
            args.append(t_own)
            in_specs.append(VMEM)
        if layer + 1 < layers:
            args += held
            in_specs += [VMEM, VMEM]
        if layer > 0:
            shapes.append(struct(plan.tokens, width))
            out_specs.append(ANY)
        if layer + 1 < layers:
            shapes += plan.gathered()
            out_specs += [ANY, ANY]
        if layer + 2 < layers:
            shapes += plan.fetched()
            out_specs += [VMEM, VMEM]
        outs = list(call(functools.partial(forward_kernel, layer, layers, plan.tokens * n_dp), "fwd", 1 + layer, args, in_specs,
                         shapes, out_specs, [wu, wd, act] + plan.sum_scratch()))
        h_cur, pre_act, act_all = take(outs, 3)
        saved.append((pre_act, act_all))
        if layer > 0:
            h_all.append(take(outs, 1))
        if layer + 1 < layers:
            weights.append(take(outs, 2))
        held = outs
    g_cur = h_cur
    grads = [None] * layers
    terms = None
    for layer in reversed(range(layers)):
        pre_act, act_all = saved[layer]
        args, in_specs = [g_cur, pre_act, w_up, w_down, *weights[layer]], [VMEM, VMEM] + [ANY] * 4
        shapes, out_specs = [struct(plan.tokens, plan.cols), struct(plan.tokens, width)], [ANY, ANY]
        scratch = [wd, act]
        if layer > 0:
            shapes.append(struct(rows, width))
            out_specs.append(VMEM)
            scratch += [wu] + plan.sum_scratch()
        if terms is not None:
            args += terms
            in_specs += [ANY] * 4
            shapes += plan.grad_outs()
            out_specs += [ANY, ANY]
            scratch += plan.grad_scratch()
        outs = list(call(functools.partial(backward_kernel, layer, layers), "bwd", 1 + layers + layer, args, in_specs, shapes,
                         out_specs, scratch))
        du_all, g_all = take(outs, 2)
        if layer > 0:
            g_cur = take(outs, 1)
        if terms is not None:
            grads[layer + 1] = take(outs, 2)
        terms = [act_all, g_all, h_all[layer], du_all]
    grads[0] = call(last_kernel, "last", 1 + 2 * layers, terms, [ANY] * 4, plan.grad_outs(), [ANY, ANY], plan.grad_scratch())
    up = jnp.stack([g[0].reshape(width, plan.cols) for g in grads])
    down = jnp.stack([g[1].reshape(plan.cols, width) for g in grads])
    return up, down


def solution(mesh):
    n_dp = mesh.shape["dp"]

    def grad_step(hidden_in, targets, w_up, w_down):
        step_fn = functools.partial(local_step, n_dp=n_dp)
        mapped = jax.shard_map(step_fn, mesh=mesh, in_specs=(P("dp", None), P("dp", None), P(None, None, "tp"), P(None, "tp", None)), out_specs=(P(None, None, "tp"), P(None, "tp", None)), check_vma=False)
        return mapped(hidden_in, targets, w_up, w_down)

    return grad_step
```

time: 1760 us -> 572 us (0.33)
  waiting for transfers between devices: 828 us -> 0 us
  blocking collectives: 747 us -> 0 us
  Pallas kernels: 0 us -> 555 us
  matrix products: 102 us -> 0 us
  other arithmetic: 47.7 us -> 10.2 us
    psum x4 -> x0, waiting for transfers between devices: 828 us -> none  [the longest x3 641 us: local_step(): lax.psum(back_part, 'tp')]
    psum x4 -> x0, blocking collectives: 747 us -> none  [local_step(): branch = lax.psum(part_out, 'tp').astype(jnp.bfloat16)]
    pallas_call x0 -> x10, Pallas kernels: none -> 555 us  [call(): pl.pallas_call(kernel, out_shape=outs, in_specs=in_specs, out_specs=out_s...]
    dot_general x22 -> x0, matrix products: 102 us -> none  [the longest x4 24 us: local_step(): jnp.dot(act_val, w_down[layer], preferred_element_type=jnp.float32)]
    convert_element_type x3 -> x0, other arithmetic: 19.8 us -> none  [the longest x2 12.1 us: local_step(): (g_cur.astype(jnp.float32) + lax.psum(back_part, 'tp')).astype(jnp.bfloat16)]
  transfers between devices with their start and end apart: 4 -> 0, of which waited for: 4 -> 0; matrix products, arithmetic and copies ran while one was open for 1% -> 0% of each run, Pallas kernels for 0% -> 0%
where the time goes in v2:
time: 572 us
  Pallas kernels  555 us (97%)
  other arithmetic  10.2 us (2%)
    pallas_call x10, Pallas kernels, call(): pl.pallas_call(kernel, out_shape=outs, in_specs=in_specs, out_specs=out_s...  555 us

profile of v2, /device:TPU:1, one launch (start us, length us, event | category | flops | bytes accessed | tf_op | source)
XLA Modules:
  0.0 571.8 jit_solution(13566817608493632666)
XLA Ops:
  0.6 1.6 constant_dynamic-slice_fusion.refs_5_
  2.2 2.3 constant_dynamic-slice_fusion.1.refs_0_
  4.5 50.1 %start.1 = (bf16[3,2048,256]{2,1,0:T(8,128)(2,1)}, bf16[8,768,256]{2,1,0:T(8,128)(2,1)}, bf16[3,256,256]{2,1,0:T(8,128)(2,1)}, bf16[768,256]{1,0:T(8,128)(2,1)}) custom-call(bf16[4,2048,256]{2,1,0:T(8,128)(2,1)} %refs_2_.16, bf16[4,256,2048]{2,1,0:T(8,128)(2,1)} %refs_3_.7), custom_call_target="tpu_custom_call" | custom-call | flops 40000000000 | bytes 20000000 | tf_op jit(solution)/shard_map/start/pallas_call | solution.py:588
  54.7 52.5 %fwd.4 = (bf16[256,2048]{1,0:T(8,128)(2,1)}, bf16[256,1024]{1,0:T(8,128)(2,1)}, bf16[1024,256]{1,0:T(8,128)(2,1)}, bf16[3,2048,256]{2,1,0:T(8,128)(2,1)}, bf16[8...) custom-call(bf16[256,2048]{1,0:T(8,128)(2,1)} %constant_dynamic-slice_fusion.1.refs_0_, ...), custom_call_target="tpu_custom_call" | custom-call | flops 40000000000 | bytes 20000000 | tf_op jit(solution)/shard_map/fwd/pallas_call | solution.py:588
  107.1 59.9 %fwd.5 = (bf16[256,2048]{1,0:T(8,128)(2,1)}, bf16[256,1024]{1,0:T(8,128)(2,1)}, bf16[1024,256]{1,0:T(8,128)(2,1)}, bf16[1024,2048]{1,0:T(8,128)(2,1)}, bf16[3,20...) custom-call(bf16[256,2048]{1,0:T(8,128)(2,1)} %get-tuple-element.55., ...), custom_call_target="tpu_custom_call" | custom-call | flops 40000000000 | bytes 20000000 | tf_op jit(solution)/shard_map/fwd/pallas_call | solution.py:588
  167.0 50.3 %fwd.6 = (bf16[256,2048]{1,0:T(8,128)(2,1)}, bf16[256,1024]{1,0:T(8,128)(2,1)}, bf16[1024,256]{1,0:T(8,128)(2,1)}, bf16[1024,2048]{1,0:T(8,128)(2,1)}, bf16[3,20...) custom-call(bf16[256,2048]{1,0:T(8,128)(2,1)} %get-tuple-element.60.refs_0_, bf16[4,2048,256]{2,1,0:T(8,128)(2,1)} %refs_2_.16, ...), custom_call_target="tpu_custom_call" | custom-call | flops 40000000000 | bytes 20000000 | tf_op jit(solution)/shard_map/fwd/pallas_call | solution.py:588
  217.3 46.9 %fwd.7 = (bf16[256,2048]{1,0:T(8,128)(2,1)}, bf16[256,1024]{1,0:T(8,128)(2,1)}, bf16[1024,256]{1,0:T(8,128)(2,1)}, bf16[1024,2048]{1,0:T(8,128)(2,1)}) custom-call(bf16[256,2048]{1,0:T(8,128)(2,1)} %get-tuple-element.65.refs_0_, bf16[4,2048,256]{2,1,0:T(8,128)(2,1)} %refs_2_.16, bf16[4,256,2048]{2,1,0:T(8,128)(2,1)} %refs_3_.7, ...), custom_call_target="tpu_custom_call" | custom-call | flops 40000000000 | bytes 20000000 | tf_op jit(solution)/shard_map/fwd/pallas_call | solution.py:588
  264.2 46.2 %bwd.4 = (bf16[1024,256]{1,0:T(8,128)(2,1)}, bf16[1024,2048]{1,0:T(8,128)(2,1)}, bf16[256,2048]{1,0:T(8,128)(2,1)}) custom-call(bf16[256,2048]{1,0:T(8,128)(2,1)} %get-tuple-element.68.refs_0_, bf16[256,1024]{1,0:T(8,128)(2,1)} %get-tuple-element.69.refs_1_, bf16[4,2048,256]{2,1,0:T(8,128)(2,1)} %refs_2_.16, bf16[4,256,2048]{2,1,0:T(8,128)(2,1)} %refs_3_.7, ...), custom_call_target="tpu_custom_call" | custom-call | flops 40000000000 | bytes 20000000 | tf_op jit(solution)/shard_map/bwd/pallas_call | solution.py:588
  310.5 69.4 %bwd.5 = (bf16[1024,256]{1,0:T(8,128)(2,1)}, bf16[1024,2048]{1,0:T(8,128)(2,1)}, bf16[256,2048]{1,0:T(8,128)(2,1)}, f32[4,2,256,256]{3,2,1,0:T(8,128)}, f32[4,2,32,2048]{3,2,1,0:T(8,128)}) custom-call(bf16[256,2048]{1,0:T(8,128)(2,1)} %get-tuple-element.70.refs_0_, bf16[256,1024]{1,0:T(8,128)(2,1)} %get-tuple-element.71.refs_1_, ...), custom_call_target="tpu_custom_call" | custom-call | flops 40000000000 | bytes 20000000 | tf_op jit(solution)/shard_map/bwd/pallas_call | solution.py:588
  379.9 68.9 %bwd.6 = (bf16[1024,256]{1,0:T(8,128)(2,1)}, bf16[1024,2048]{1,0:T(8,128)(2,1)}, bf16[256,2048]{1,0:T(8,128)(2,1)}, f32[4,2,256,256]{3,2,1,0:T(8,128)}, f32[4,2,32,2048]{3,2,1,0:T(8,128)}) custom-call(bf16[256,2048]{1,0:T(8,128)(2,1)} %get-tuple-element.76.refs_0_, bf16[256,1024]{1,0:T(8,128)(2,1)} %get-tuple-element.77.refs_1_, ...), custom_call_target="tpu_custom_call" | custom-call | flops 40000000000 | bytes 20000000 | tf_op jit(solution)/shard_map/bwd/pallas_call | solution.py:588
  448.8 57.2 %bwd.7 = (bf16[1024,256]{1,0:T(8,128)(2,1)}, bf16[1024,2048]{1,0:T(8,128)(2,1)}, f32[4,2,256,256]{3,2,1,0:T(8,128)}, f32[4,2,32,2048]{3,2,1,0:T(8,128)}) custom-call(bf16[256,2048]{1,0:T(8,128)(2,1)} %get-tuple-element.82.refs_0_, bf16[256,1024]{1,0:T(8,128)(2,1)} %get-tuple-element.83.refs_1_, bf16[4,2048,256]{2,1,0:T(8,128)(2,1)} %refs_2_.16, ...), custom_call_target="tpu_custom_call" | custom-call | flops 40000000000 | bytes 20000000 | tf_op jit(solution)/shard_map/bwd/pallas_call | solution.py:588
  506.1 0.0 copy-start.1
  506.1 53.8 %last.1 = (f32[4,2,256,256]{3,2,1,0:T(8,128)}, f32[4,2,32,2048]{3,2,1,0:T(8,128)}) custom-call(bf16[1024,256]{1,0:T(8,128)(2,1)} %get-tuple-element.54.refs_0_, bf16[1024,2048]{1,0:T(8,128)(2,1)} %get-tuple-element.88.refs_1_, bf16[1024,2048]{1,0:T(8,128)(2,1)} %refs_2_.17, bf16[1024,256]{1,0:T(8,128)(2,1)} %get-tuple-element.89.refs_3_), custom_call_target="tpu_custom_call" | custom-call | flops 40000000000 | bytes 20000000 | tf_op jit(solution)/shard_map/last/pallas_call | solution.py:588
  559.9 0.0 copy-done.1
  559.9 0.0 copy-start
  559.9 0.0 copy-start.2
  559.9 0.0 copy-start.3
  559.9 0.0 copy-start.4
  559.9 6.5 %pad_maximum_fusion = f32[4,2048,256]{2,1,0:T(8,128)} fusion(f32[1,2048,256]{2,1,0:T(8,128)S(1)} %bitcast.9, f32[1,2048,256]{2,1,0:T(8,128)} %bitcast.11, f32[1,2048,256]{2,1,0:T(8,128)} %bitcast.13, f32[1,2048,256]{2,1,0:T(8,128)} %bitcast.15), kind=kLoop, calls=%fused_computation | loop fusion | flops 6291456 | bytes 16777216 | tf_op jit(solution)/shard_map/stack | solution.py:702
  566.5 0.0 copy-done
  566.5 0.0 copy-done.2
  566.5 1.1 copy-done.3
  567.6 0.6 copy-done.4
  568.2 3.7 pad_maximum_fusion.1
Async XLA Ops:
  506.1 53.8 %copy-start.1 = (f32[4,2,256,256]{3,2,1,0:T(8,128)S(1)}, f32[4,2,256,256]{3,2,1,0:T(8,128)}, u32[]{:S(2)}) copy-start(f32[4,2,256,256]{3,2,1,0:T(8,128)} %get-tuple-element.93) | copy-start | bytes 6291460
  559.9 6.6 %copy-start = (f32[4,2,32,2048]{3,2,1,0:T(8,128)S(1)}, f32[4,2,32,2048]{3,2,1,0:T(8,128)}, u32[]{:S(2)}) copy-start(f32[4,2,32,2048]{3,2,1,0:T(8,128)} %get-tuple-element.97) | copy-start | bytes 6291460
  559.9 6.6 %copy-start.2 = (f32[4,2,32,2048]{3,2,1,0:T(8,128)S(1)}, f32[4,2,32,2048]{3,2,1,0:T(8,128)}, u32[]{:S(2)}) copy-start(f32[4,2,32,2048]{3,2,1,0:T(8,128)} %get-tuple-element.96) | copy-start | bytes 6291460
  559.9 7.6 %copy-start.3 = (f32[4,2,32,2048]{3,2,1,0:T(8,128)S(1)}, f32[4,2,32,2048]{3,2,1,0:T(8,128)}, u32[]{:S(2)}) copy-start(f32[4,2,32,2048]{3,2,1,0:T(8,128)} %get-tuple-element.95) | copy-start | bytes 6291460
  559.9 8.2 %copy-start.4 = (f32[4,2,32,2048]{3,2,1,0:T(8,128)S(1)}, f32[4,2,32,2048]{3,2,1,0:T(8,128)}, u32[]{:S(2)}) copy-start(f32[4,2,32,2048]{3,2,1,0:T(8,128)} %get-tuple-element.94) | copy-start | bytes 6291460

commit v3 on v0

v3 whole, which is shorter than its diff:
```python
import functools
import jax
import jax.numpy as jnp
from jax import lax
from jax.experimental import pallas as pl
from jax.experimental.pallas import tpu as pltpu
from jax.sharding import PartitionSpec as P

NZ, NY, NX = 8, 4, 4
COPIES, LOCALS = 512, 160
ROW_CONTRACT = (((0,), (0,)), ((), ()))
COL_CONTRACT = (((1,), (1,)), ((), ()))
Z_CHAINS = ((0, 0, 4), (1, 0, 3), (1, 1, 4), (0, 1, 3))
X_CHAINS = ((0, 0, 2), (1, 0, 1), (1, 1, 2), (0, 1, 1))
ANY = pl.BlockSpec(memory_space=pl.ANY)
VMEM = pl.BlockSpec(memory_space=pltpu.VMEM)
BF16, F32 = jnp.bfloat16, jnp.float32


def gelu_tanh(value):
    return jax.nn.gelu(value, approximate=True)


def at(start, size):
    return pl.ds(pl.multiple_of(start, size), size)


def shift(position, amount, size):
    return lax.rem(position + amount % size, size)


class Net:
    def __init__(self, send_sem, recv_sem, local_sem):
        tp, dp = lax.axis_index("tp"), lax.axis_index("dp")
        self.z, self.y = lax.div(tp, NY), lax.rem(tp, NY)
        self.x, self.c = lax.div(dp, 2), lax.rem(dp, 2)
        self.send_sem, self.recv_sem, self.local_sem = send_sem, recv_sem, local_sem
        self.n_copies = self.n_locals = 0

    def device(self, dz=0, dy=0, dx=0, other_core=False):
        z, y, x = shift(self.z, dz, NZ), shift(self.y, dy, NY), shift(self.x, dx, NX)
        c = 1 - self.c if other_core else self.c
        return {"tp": z * NY + y, "dp": x * 2 + c}

    def barrier(self):
        peers = [self.device(dy=s) for s in (1, 2, 3)] + [self.device(dz=s) for s in (1, -1)]
        peers += [self.device(dx=s) for s in (1, -1)] + [self.device(other_core=True)]
        sem = pltpu.get_barrier_semaphore()
        for peer in peers:
            pl.semaphore_signal(sem, inc=1, device_id=peer, device_id_type=pl.DeviceIdType.MESH)
        pl.semaphore_wait(sem, len(peers))

    def copy(self, src, dst, **where):
        index = self.n_copies
        self.n_copies += 1
        return pltpu.make_async_remote_copy(
            src_ref=src, dst_ref=dst, send_sem=self.send_sem.at[index], recv_sem=self.recv_sem.at[index],
            device_id=self.device(**where), device_id_type=pl.DeviceIdType.MESH)

    def local(self, src, dst):
        index = self.n_locals
        self.n_locals += 1
        return pltpu.make_async_copy(src, dst, self.local_sem.at[index])


class RowGather:
    def __init__(self, net, block, out):
        rows = block.shape[0]
        half = rows // 2
        below, above = shift(net.y, -1, NY), shift(net.y, 1, NY)
        own = out.at[at(net.y * rows, rows)]
        lower, upper = out.at[at(below * rows, half)], out.at[at(above * rows + half, half)]
        self.local = net.local(block, own)
        self.first = [net.copy(block, own, dy=1), net.copy(block, own, dy=-1)]
        self.second = [net.copy(lower, lower, dy=1), net.copy(upper, upper, dy=-1)]

    def start(self):
        self.local.start()
        for copy in self.first:
            copy.start()

    def relay(self):
        for copy, onward in zip(self.first, self.second):
            copy.wait_recv()
            onward.start()

    def sent(self):
        self.local.wait()
        for copy in self.first:
            copy.wait_send()

    def finish(self):
        for copy in self.second:
            copy.wait()


class ColumnExchange:
    def __init__(self, net, block, out):
        rows, cols = block.shape[0], block.shape[1] // NY
        own = out.at[at(net.y * rows, rows)]
        self.local = net.local(block.at[:, 0:cols], own)
        self.copies = [net.copy(block.at[:, s * cols:(s + 1) * cols], own, dy=s) for s in (1, 3, 2)]

    def start(self):
        self.local.start()
        for copy in self.copies:
            copy.start()

    def finish(self):
        self.local.wait()
        for copy in self.copies:
            copy.wait()


class PieceFetch:
    def __init__(self, net, piece, slot):
        self.copies = [net.copy(piece, slot(NY - s - 1), dy=s) for s in (1, 3, 2)]

    def start(self):
        for copy in self.copies:
            copy.start()

    def arrived(self):
        for copy in self.copies:
            copy.wait_recv()

    def sent(self):
        for copy in self.copies:
            copy.wait_send()


class PieceSpread:
    def __init__(self, net, held, view):
        own = view(0, None)
        self.local = net.local(held, own)
        self.first = [net.copy(held, own, dx=d) for d in (1, -1)]
        self.second = [net.copy(view(-d, half), view(-d, half), dx=d) for half, d in ((0, 1), (1, -1))]
        self.across = [net.copy(held, own, other_core=True)]
        self.across += [net.copy(view(d, None), view(d, None), other_core=True) for d in (-1, 1, 2)]

    def start(self):
        for copy in (self.local, *self.first, self.across[0]):
            copy.start()

    def relay(self):
        for first, second, across in zip(self.first, self.second, self.across[1:3]):
            first.wait_recv()
            second.start()
            across.start()

    def cross(self):
        for copy in self.second:
            copy.wait_recv()
        self.across[3].start()

    def finish(self):
        self.local.wait()
        for copy in (*self.first, *self.second):
            copy.wait_send()
        for copy in self.across:
            copy.wait()


class Ring:
    def __init__(self, net, axis, chains, part, slot, out):
        self.net, self.axis, self.chains = net, axis, chains
        self.size = {"x": NX, "z": NZ}[axis]
        self.here = {"x": net.x, "z": net.z}[axis]
        self.part, self.slot, self.out = part, slot, out
        self.copies, self.last = [], {}

    def owner(self, direction, amount):
        return shift(self.here, amount if direction == 0 else -amount, self.size)

    def send(self, chain, src, dst):
        direction = self.chains[chain][0]
        copy = self.net.copy(src, dst, **{"d" + self.axis: 1 if direction == 0 else -1})
        copy.start()
        self.copies.append(copy)
        self.last[chain] = copy

    def reduce(self, chain, step):
        direction, half, hops = self.chains[chain]
        if step >= hops:
            return
        mine = self.part(self.owner(direction, hops - step), half)
        if step > 0:
            self.last[chain].wait_recv()
            mine[...] = mine[...] + self.slot(chain, step - 1)[...]
        self.send(chain, mine, self.slot(chain, step))

    def reduce_half(self, half):
        for chain, (_, h, _) in enumerate(self.chains):
            if h == half:
                self.reduce(chain, 0)

    def reduce_all(self, step):
        for chain in range(len(self.chains)):
            self.reduce(chain, step)

    def total(self, half):
        value = self.part(self.here, half)[...]
        for chain, (_, h, hops) in enumerate(self.chains):
            if h == half:
                self.last[chain].wait_recv()
                value = value + self.slot(chain, hops - 1)[...]
        return value

    def gather(self, chain, step, first=None):
        direction, half, hops = self.chains[chain]
        if step >= hops:
            return
        if step > 0:
            self.last[chain].wait_recv()
        held = self.out(self.owner(direction, -step), half)
        self.send(chain, held if first is None else first, held)

    def gather_half(self, half):
        for chain, (_, h, _) in enumerate(self.chains):
            if h == half:
                self.gather(chain, 0)

    def gather_all(self, step):
        for chain in range(len(self.chains)):
            self.gather(chain, step)

    def arrived(self):
        for copy in self.last.values():
            copy.wait_recv()

    def finish(self):
        for copy in self.copies:
            copy.wait_send()


def slot_index(chains, chain, step):
    return sum(hops for _, _, hops in chains[:chain]) + step


def z_ring(net, part, slots, out):
    rows, cols = part.shape[0] // NZ, part.shape[1] // 2

    def block(ref):
        return lambda owner, half: ref.at[at(owner * rows, rows), half * cols:(half + 1) * cols]

    ring = Ring(net, "z", Z_CHAINS, block(part), lambda chain, step: slots.at[slot_index(Z_CHAINS, chain, step)], block(out))
    ring.block = block
    return ring


class GradSum:
    def __init__(self, net, part, sib, slots, out):
        self.net, self.mine, self.sib, self.out = net, part, sib, out
        half_rows = part.shape[2] // 2

        def block(ref):
            return lambda owner, half: ref.at[owner, net.c, half * half_rows:(half + 1) * half_rows]

        self.ring = Ring(net, "x", X_CHAINS, block(part), lambda chain, step: slots.at[slot_index(X_CHAINS, chain, step)], block(out))
        self.swap = net.copy(part.at[:, 1 - net.c], sib, other_core=True)
        self.across, self.local = [], []

    def merge(self):
        c = self.net.c
        self.swap.wait_recv()
        for k in range(NX):
            self.mine[k, c] = self.mine[k, c] + self.sib[k]
        for half in (0, 1):
            self.ring.reduce_half(half)

    def step(self):
        self.ring.reduce_all(1)

    def cross(self, src, dst):
        copy = self.net.copy(src, dst, other_core=True)
        copy.start()
        self.across.append(copy)

    def settle(self):
        for half in (0, 1):
            own = self.ring.part(self.net.x, half)
            own[...] = self.ring.total(half)
            for chain, (_, h, _) in enumerate(X_CHAINS):
                if h == half:
                    self.ring.gather(chain, 0, own)
        x, c = self.net.x, self.net.c
        self.local = self.net.local(self.mine.at[x, c], self.out.at[x, c])
        self.local.start()
        self.cross(self.mine.at[x, c], self.out.at[x, c])

    def relay(self):
        self.ring.gather_all(1)

    def finish(self):
        self.ring.arrived()
        for dx in (1, -1, 2):
            held = self.out.at[shift(self.net.x, dx, NX), self.net.c]
            self.cross(held, held)
        self.local.wait()
        self.swap.wait_send()
        self.ring.finish()

    def end(self):
        for copy in self.across:
            copy.wait()


def take(refs, count):
    taken = refs[:count]
    del refs[:count]
    return taken if count > 1 else taken[0]


def step_kernel(layers, total_tokens, *refs):
    refs = list(refs)
    h0_ref, t_ref, w_up, w_down, x_all = take(refs, 5)
    grad_up, grad_down = take(refs, 2)
    all_up, all_down, h_all, a_all, g_all, du_all = take(refs, 6)
    wu, wd, rows_buf, u_buf, act, dpre, part, slots = take(refs, 8)
    held_up, held_down = take(refs, 2)
    up_part, up_sib, up_slots, down_part, down_sib, down_slots = take(refs, 6)
    a_in, g_in, h_in, du_in = take(refs, 4)
    net = Net(*refs)
    top = layers - 1
    width, hidden = wu.shape[1], wu.shape[2]
    cols = hidden // NY
    piece = held_up.shape[2]
    tile = width // 8
    dp = net.x * 2 + net.c

    def start(copies):
        for copy in copies:
            copy.start()

    def wait(copies):
        for copy in copies:
            copy.wait()

    def fetch_of(layer):
        return (PieceFetch(net, w_up.at[layer, at(dp * piece, piece)], lambda slot: held_up.at[layer, slot]),
                PieceFetch(net, w_down.at[layer, :, at(dp * piece, piece)], lambda slot: held_down.at[layer, slot * cols:(slot + 1) * cols]))

    def spread_of(layer):
        def up_view(dx, half):
            first = (shift(net.x, dx, NX) * 2 + net.c) * piece
            if half is None:
                return all_up.at[layer, :, at(first, piece)]
            return all_up.at[layer, :, at(first + half * (piece // 2), piece // 2)]

        def down_view(dx, half):
            index, tall = shift(net.x, dx, NX) * 2 + net.c, 3 * cols
            if half is None:
                return all_down.at[layer, index]
            return all_down.at[layer, index, half * (tall // 2):(half + 1) * (tall // 2)]

        return PieceSpread(net, held_up.at[layer], up_view), PieceSpread(net, held_down.at[layer], down_view)

    def up_loads(layer):
        b = layer % 2
        own = net.local(w_up.at[layer], wu.at[b, :, 0:cols])
        return own, [net.local(all_up.at[layer, s], wu.at[b, :, (s + 1) * cols:(s + 2) * cols]) for s in range(NY - 1)]

    def down_loads(layer):
        b = layer % 2
        own = net.local(w_down.at[layer], wd.at[b, 0:cols])
        return own, [net.local(all_down.at[layer, n], wd.at[b, cols:, n * piece:(n + 1) * piece]) for n in range(all_down.shape[1])]

    net.barrier()
    fetches = [fetch_of(0)]
    start(fetches[0])
    fetches.append(fetch_of(1))
    start(fetches[1])
    loads = up_loads(0), down_loads(0)
    loads[0][0].start()
    loads[1][0].start()
    first = net.local(h0_ref, rows_buf.at[0])
    first.start()
    spread_up, spread_down = spread_of(0)
    fetches[0][0].arrived()
    spread_up.start()
    fetches[0][1].arrived()
    spread_down.start()
    spread_up.relay()
    spread_down.relay()
    spread_up.cross()
    spread_up.finish()
    start(loads[0][1])
    first.wait()

    rows = None
    for layer in range(layers):
        b = layer % 2
        h_ref, out_ref = rows_buf.at[b], rows_buf.at[1 - b]
        spreads = None
        if layer > 0:
            rows = RowGather(net, h_ref, h_all.at[layer - 1])
            rows.start()
            if layer < top:
                fetches[layer + 1][0].arrived()
                fetches[layer + 1][1].arrived()
                spreads = spread_of(layer + 1)
                start(spreads)
        loads[0][0].wait()
        wait(loads[0][1])

        @pl.loop(0, NY)
        def _(n):
            block = at(n * cols, cols)
            pre = jnp.dot(h_ref[...], wu[b, :, block], preferred_element_type=F32).astype(BF16)
            u_buf[layer, :, block] = pre
            act[:, block] = gelu_tanh(pre.astype(F32)).astype(BF16)

        exchange = ColumnExchange(net, act, a_all.at[layer])
        if layer == 0:
            exchange.start()
            spread_down.cross()
            spread_down.finish()
            start(loads[1][1])
            fetches[1][0].arrived()
            fetches[1][1].arrived()
            spreads = spread_of(1)
            start(spreads)
        ring = z_ring(net, part, slots, out_ref)

        def down(n):
            part[:, at(n * tile, tile)] = jnp.dot(act[...], wd[b, :, at(n * tile, tile)], preferred_element_type=F32)

        loads[1][0].wait()
        wait(loads[1][1])
        pl.loop(0, 4)(down)
        ring.reduce_half(0)
        pl.loop(4, 8)(down)
        ring.reduce_half(1)
        if layer == 0:
            for ahead in range(2, layers):
                fetches.append(fetch_of(ahead))
                start(fetches[ahead])
        else:
            exchange.start()
        for step in (1, 2, 3):
            ring.reduce_all(step)
        for half in (0, 1):
            value = ring.block(h_ref)(net.z, half)[...] + ring.total(half).astype(BF16)
            if layer == top:
                wide = value.shape[1]
                err = value.astype(F32) - t_ref[:, half * wide:(half + 1) * wide].astype(F32)
                value = (err / total_tokens).astype(BF16)
            ring.out(net.z, half)[...] = value
            ring.gather_half(half)
        if spreads:
            spreads[0].relay()
            spreads[1].relay()
        ring.gather_all(1)
        if layer > 0:
            rows.relay()
        ring.gather_all(2)
        if spreads:
            spreads[0].cross()
            spreads[1].cross()
        ring.gather_all(3)
        if spreads:
            spreads[0].finish()
            spreads[1].finish()
            loads = up_loads(layer + 1), down_loads(layer + 1)
            for own, others in loads:
                own.start()
                start(others)
        if layer > 0:
            rows.sent()
        exchange.finish()
        ring.arrived()
        ring.finish()
        if layer > 0:
            rows.finish()
    for pair in fetches:
        pair[0].sent()
        pair[1].sent()

    def up_product():
        tall = up_part.shape[2]

        @pl.loop(0, 2 * NX)
        def _(n):
            up_part[lax.div(n, 2), lax.rem(n, 2)] = lax.dot_general(
                h_in[:, at(n * tall, tall)], du_in[...], ROW_CONTRACT, preferred_element_type=F32)

    def down_product():
        @pl.loop(0, 8)
        def _(n):
            block = at(n * tile, tile)
            value = lax.dot_general(a_in[...], g_in[:, block], ROW_CONTRACT, preferred_element_type=F32)
            down_part[:, :, :, block] = value.reshape(NX, 2, cols // 8, tile)

    def up_sum_of(layer):
        return GradSum(net, up_part, up_sib, up_slots, grad_up.at[layer])

    def down_sum_of(layer):
        return GradSum(net, down_part, down_sib, down_slots, grad_down.at[layer])

    reload, last_rows, last_up = {}, None, None
    for layer in reversed(range(layers)):
        b = layer % 2
        g_ref, out_ref = rows_buf.at[1 - b], rows_buf.at[b]
        h_load = net.local(x_all if layer == 0 else h_all.at[layer - 1], h_in)
        a_load = net.local(a_all.at[layer], a_in)
        if layer in reload:
            reload[layer][0][0].wait()
            wait(reload[layer][0][1])

        @pl.loop(0, NY)
        def _(n):
            block = at(n * cols, cols)
            d_act = lax.dot_general(g_ref[...], wd[b, block, :], COL_CONTRACT, preferred_element_type=F32)
            _, gelu_vjp = jax.vjp(gelu_tanh, u_buf[layer, :, block].astype(F32))
            dpre[:, block] = gelu_vjp(d_act)[0].astype(BF16)

        exchange = ColumnExchange(net, dpre, du_all.at[layer])
        rows = RowGather(net, g_ref, g_all.at[layer])
        ring = None
        if layer == 0:
            exchange.start()
            rows.start()
        else:
            if layer in reload:
                reload[layer][1][0].wait()
                wait(reload[layer][1][1])
            ring = z_ring(net, part, slots, out_ref)

            def back(n):
                part[:, at(n * tile, tile)] = lax.dot_general(
                    dpre[...], wu[b, at(n * tile, tile), :], COL_CONTRACT, preferred_element_type=F32)

            pl.loop(0, 4)(back)
            ring.reduce_half(0)
            exchange.start()
            rows.start()
            pl.loop(4, 8)(back)
            ring.reduce_half(1)
        down_sum = None
        if last_rows is not None:
            last_rows.finish()
            g_load = net.local(g_all.at[layer + 1], g_in)
            g_load.start()
            last_up.relay()
        if layer >= 2:
            reload[layer - 2] = (down_loads(layer - 2), up_loads(layer - 2)) if layer > 2 else (down_loads(0),)
            for own, others in reload[layer - 2]:
                own.start()
                start(others)
        if last_rows is not None:
            g_load.wait()
            last_a.wait()
            down_sum = down_sum_of(layer + 1)
            down_product()
            down_sum.swap.start()
        a_load.start()
        h_load.start()
        if ring:
            ring.reduce_all(1)
        if down_sum:
            last_up.finish()
            down_sum.merge()
        if ring:
            ring.reduce_all(2)
        if down_sum:
            last_up.end()
        exchange.finish()
        du_load = net.local(du_all.at[layer], du_in)
        du_load.start()
        h_load.wait()
        du_load.wait()
        up_sum = up_sum_of(layer)
        up_product()
        up_sum.swap.start()
        if ring:
            ring.reduce_all(3)
        if down_sum:
            down_sum.step()
        if ring:
            for half in (0, 1):
                total = ring.total(half)
                ring.out(net.z, half)[...] = (ring.block(g_ref)(net.z, half)[...].astype(F32) + total).astype(BF16)
                ring.gather_half(half)
        up_sum.merge()
        if ring:
            ring.gather_all(1)
        rows.relay()
        if down_sum:
            down_sum.settle()
        if ring:
            ring.gather_all(2)
        up_sum.step()
        if ring:
            ring.gather_all(3)
        rows.sent()
        if down_sum:
            down_sum.relay()
        if ring:
            ring.arrived()
            ring.finish()
        if layer > 0:
            up_sum.settle()
        if down_sum:
            down_sum.finish()
            down_sum.end()
        last_rows, last_up, last_a = rows, up_sum, a_load
    last_up.settle()
    last_rows.finish()
    g_load = net.local(g_all.at[0], g_in)
    g_load.start()
    last_up.relay()
    g_load.wait()
    last_a.wait()
    down_sum = down_sum_of(0)
    down_product()
    down_sum.swap.start()
    last_up.finish()
    down_sum.merge()
    down_sum.step()
    down_sum.settle()
    down_sum.relay()
    last_up.end()
    down_sum.finish()
    down_sum.end()


def local_step(hidden, targets, w_up, w_down, n_dp):
    layers, width, cols = w_up.shape
    tokens = hidden.shape[0]
    rows, inner, piece = tokens // NY, cols * NY, width // n_dp
    tp = lax.axis_index("tp")
    z, y = lax.div(tp, NY), lax.rem(tp, NY)
    h_own = lax.dynamic_slice(hidden, (y * rows, 0), (rows, width))
    t_own = lax.dynamic_slice(targets, (y * rows + z * (rows // NZ), 0), (rows // NZ, width))
    up_shape, down_shape = (NX, 2, width // 8, cols), (NX, 2, cols // 8, width)

    def out(dtype, *shape):
        return jax.ShapeDtypeStruct(shape, dtype)

    outs = [out(F32, layers, *up_shape), out(F32, layers, *down_shape),
            out(BF16, layers, NY - 1, width, cols), out(BF16, layers, n_dp, (NY - 1) * cols, piece),
            out(BF16, layers - 1, tokens, width), out(BF16, layers, tokens, cols),
            out(BF16, layers, tokens, width), out(BF16, layers, tokens, cols)]

    def sum_scratch(shape):
        return [pltpu.VMEM(shape, F32), pltpu.VMEM((NX, *shape[2:]), F32), pltpu.VMEM((6, shape[2] // 2, shape[3]), F32)]

    scratch = [pltpu.VMEM((2, width, inner), BF16), pltpu.VMEM((2, inner, width), BF16), pltpu.VMEM((2, rows, width), BF16),
               pltpu.VMEM((layers, rows, inner), BF16), pltpu.VMEM((rows, inner), BF16), pltpu.VMEM((rows, inner), BF16),
               pltpu.VMEM((rows, width), F32), pltpu.VMEM((14, rows // NZ, width // 2), F32),
               pltpu.VMEM((layers, NY - 1, piece, cols), BF16), pltpu.VMEM((layers, (NY - 1) * cols, piece), BF16),
               *sum_scratch(up_shape), *sum_scratch(down_shape),
               pltpu.VMEM((tokens, cols), BF16), pltpu.VMEM((tokens, width), BF16), pltpu.VMEM((tokens, width), BF16), pltpu.VMEM((tokens, cols), BF16),
               pltpu.SemaphoreType.DMA((COPIES,)), pltpu.SemaphoreType.DMA((COPIES,)), pltpu.SemaphoreType.DMA((LOCALS,))]
    up, down = pl.pallas_call(
        functools.partial(step_kernel, layers, tokens * n_dp), out_shape=outs, in_specs=[ANY, VMEM, ANY, ANY, ANY],
        out_specs=[ANY] * len(outs), scratch_shapes=scratch, name="step",
        compiler_params=pltpu.CompilerParams(collective_id=0, has_side_effects=True, vmem_limit_bytes=60 * 1024 * 1024),
    )(h_own, t_own, w_up, w_down, hidden)[:2]
    return up.reshape(layers, width, cols), down.reshape(layers, cols, width)


def solution(mesh):
    n_dp = mesh.shape["dp"]

    def grad_step(hidden_in, targets, w_up, w_down):
        step_fn = functools.partial(local_step, n_dp=n_dp)
        mapped = jax.shard_map(step_fn, mesh=mesh, in_specs=(P("dp", None), P("dp", None), P(None, None, "tp"), P(None, "tp", None)), out_specs=(P(None, None, "tp"), P(None, "tp", None)), check_vma=False)
        return mapped(hidden_in, targets, w_up, w_down)

    return grad_step
```

time: 1760 us -> 474 us (0.27)
  waiting for transfers between devices: 828 us -> 0 us
  blocking collectives: 747 us -> 0 us
  Pallas kernels: 0 us -> 458 us
  matrix products: 102 us -> 0 us
  other arithmetic: 47.7 us -> 0 us
    psum x4 -> x0, waiting for transfers between devices: 828 us -> none  [the longest x3 641 us: local_step(): lax.psum(back_part, 'tp')]
    psum x4 -> x0, blocking collectives: 747 us -> none  [local_step(): branch = lax.psum(part_out, 'tp').astype(jnp.bfloat16)]
    pallas_call x0 -> x1, Pallas kernels: none -> 458 us  [local_step(): pl.pallas_call(functools.partial(step_kernel, layers, tokens * n_dp), out...]
    dot_general x22 -> x0, matrix products: 102 us -> none  [the longest x4 24 us: local_step(): jnp.dot(act_val, w_down[layer], preferred_element_type=jnp.float32)]
    convert_element_type x3 -> x0, other arithmetic: 19.8 us -> none  [the longest x2 12.1 us: local_step(): (g_cur.astype(jnp.float32) + lax.psum(back_part, 'tp')).astype(jnp.bfloat16)]
  transfers between devices with their start and end apart: 4 -> 0, of which waited for: 4 -> 0; matrix products, arithmetic and copies ran while one was open for 1% -> 0% of each run, Pallas kernels for 0% -> 0%
where the time goes in v3:
time: 474 us; the launch traced here: 473 us
  Pallas kernels  458 us (97%)
  local copies, waits for them, and re-layouts  14.9 us (3%)
    pallas_call x1, Pallas kernels, local_step(): pl.pallas_call(functools.partial(step_kernel, layers, tokens * n_dp), out...  458 us
    unnamed x4, local copies, waits for them, and re-layouts  11.1 us

profile of v3, /device:TPU:1, one launch (start us, length us, event | category | flops | bytes accessed | tf_op | source)
XLA Modules:
  0.0 473.2 jit_solution(467302061410982805)
XLA Ops:
  0.6 1.6 constant_dynamic-slice_fusion.refs_1_
  2.2 2.3 constant_dynamic-slice_fusion.1.refs_0_
  4.5 457.6 %step.1 = (f32[4,4,2,256,256]{4,3,2,1,0:T(8,128)}, f32[4,4,2,32,2048]{4,3,2,1,0:T(8,128)}, bf16[4,3,2048,256]{3,2,1,0:T(8,128)(2,1)}, bf16[4,8,768,256]{3,2,1,0:...) custom-call(bf16[256,2048]{1,0:T(8,128)(2,1)} %constant_dynamic-slic, ...), custom_call_target="tpu_custom_call" | custom-call | tf_op jit(solution)/shard_map/step/pallas_call | solution.py:655
  462.2 0.0 copy-start
  462.2 7.7 %copy.8 = f32[4,2048,256]{2,1,0:T(8,128)} copy(f32[4,2048,256]{2,1,0:T(8,128)} %bitcast.3) | data formatting | bytes 16777216
  469.8 0.0 copy-done
  469.8 3.4 copy.9
Async XLA Ops:
  462.2 7.7 %copy-start = (f32[4,4,2,32,2048]{4,3,2,1,0:T(8,128)S(1)}, f32[4,4,2,32,2048]{4,3,2,1,0:T(8,128)}, u32[]{:S(2)}) copy-start(f32[4,4,2,32,2048]{4,3,2,1,0:T(8,128)} %get-tuple-element.5) | copy-start | bytes 25165828

commit v4 on v3

--- a/solution.py
+++ b/solution.py
@@ -7,13 +7,13 @@
 from jax.sharding import PartitionSpec as P
 
 NZ, NY, NX = 8, 4, 4
-COPIES, LOCALS = 512, 160
+COPIES, LOCALS = 832, 160
+PARTS = 4
 ROW_CONTRACT = (((0,), (0,)), ((), ()))
 COL_CONTRACT = (((1,), (1,)), ((), ()))
-Z_CHAINS = ((0, 0, 4), (1, 0, 3), (1, 1, 4), (0, 1, 3))
+Z_CHAINS = tuple(chain for q in range(PARTS) for chain in ((q % 2, q, 4), (1 - q % 2, q, 3)))
 X_CHAINS = ((0, 0, 2), (1, 0, 1), (1, 1, 2), (0, 1, 1))
 ANY = pl.BlockSpec(memory_space=pl.ANY)
-VMEM = pl.BlockSpec(memory_space=pltpu.VMEM)
 BF16, F32 = jnp.bfloat16, jnp.float32
 
 
@@ -23,10 +23,6 @@
 
 def at(start, size):
     return pl.ds(pl.multiple_of(start, size), size)
-
-
-def shift(position, amount, size):
-    return lax.rem(position + amount % size, size)
 
 
 class Net:
@@ -34,13 +30,37 @@
         tp, dp = lax.axis_index("tp"), lax.axis_index("dp")
         self.z, self.y = lax.div(tp, NY), lax.rem(tp, NY)
         self.x, self.c = lax.div(dp, 2), lax.rem(dp, 2)
+        self.other = 1 - self.c
         self.send_sem, self.recv_sem, self.local_sem = send_sem, recv_sem, local_sem
         self.n_copies = self.n_locals = 0
+        self.known = {}
+
+    def near(self, axis, amount):
+        size = {"x": NX, "y": NY, "z": NZ}[axis]
+        key = axis, amount % size
+        if key not in self.known:
+            here = getattr(self, axis)
+            self.known[key] = lax.rem(here + key[1], size) if key[1] else here
+        return self.known[key]
+
+    def span(self, axis, amount, rows):
+        key = axis, amount % {"x": NX, "y": NY, "z": NZ}[axis], rows
+        if key not in self.known:
+            self.known[key] = at(self.near(axis, amount) * rows, rows)
+        return self.known[key]
+
+    def block(self, dx):
+        key = "block", dx % NX
+        if key not in self.known:
+            self.known[key] = self.near("x", dx) * 2 + self.c
+        return self.known[key]
 
     def device(self, dz=0, dy=0, dx=0, other_core=False):
-        z, y, x = shift(self.z, dz, NZ), shift(self.y, dy, NY), shift(self.x, dx, NX)
-        c = 1 - self.c if other_core else self.c
-        return {"tp": z * NY + y, "dp": x * 2 + c}
+        key = "device", dz % NZ, dy % NY, dx % NX, other_core
+        if key not in self.known:
+            c = self.other if other_core else self.c
+            self.known[key] = {"tp": self.near("z", dz) * NY + self.near("y", dy), "dp": self.near("x", dx) * 2 + c}
+        return self.known[key]
 
     def barrier(self):
         peers = [self.device(dy=s) for s in (1, 2, 3)] + [self.device(dz=s) for s in (1, -1)]
@@ -67,9 +87,8 @@
     def __init__(self, net, block, out):
         rows = block.shape[0]
         half = rows // 2
-        below, above = shift(net.y, -1, NY), shift(net.y, 1, NY)
-        own = out.at[at(net.y * rows, rows)]
-        lower, upper = out.at[at(below * rows, half)], out.at[at(above * rows + half, half)]
+        own = out.at[net.span("y", 0, rows)]
+        lower, upper = out.at[net.span("y", -1, rows)].at[0:half], out.at[net.span("y", 1, rows)].at[half:rows]
         self.local = net.local(block, own)
         self.first = [net.copy(block, own, dy=1), net.copy(block, own, dy=-1)]
         self.second = [net.copy(lower, lower, dy=1), net.copy(upper, upper, dy=-1)]
@@ -97,7 +116,7 @@
 class ColumnExchange:
     def __init__(self, net, block, out):
         rows, cols = block.shape[0], block.shape[1] // NY
-        own = out.at[at(net.y * rows, rows)]
+        own = out.at[net.span("y", 0, rows)]
         self.local = net.local(block.at[:, 0:cols], own)
         self.copies = [net.copy(block.at[:, s * cols:(s + 1) * cols], own, dy=s) for s in (1, 3, 2)]
 
@@ -106,10 +125,14 @@
         for copy in self.copies:
             copy.start()
 
-    def finish(self):
+    def sent(self):
         self.local.wait()
         for copy in self.copies:
-            copy.wait()
+            copy.wait_send()
+
+    def arrived(self):
+        for copy in self.copies:
+            copy.wait_recv()
 
 
 class PieceFetch:
@@ -164,13 +187,11 @@
 class Ring:
     def __init__(self, net, axis, chains, part, slot, out):
         self.net, self.axis, self.chains = net, axis, chains
-        self.size = {"x": NX, "z": NZ}[axis]
-        self.here = {"x": net.x, "z": net.z}[axis]
         self.part, self.slot, self.out = part, slot, out
         self.copies, self.last = [], {}
 
     def owner(self, direction, amount):
-        return shift(self.here, amount if direction == 0 else -amount, self.size)
+        return amount if direction == 0 else -amount
 
     def send(self, chain, src, dst):
         direction = self.chains[chain][0]
@@ -194,12 +215,21 @@
             if h == half:
                 self.reduce(chain, 0)
 
-    def reduce_all(self, step):
-        for chain in range(len(self.chains)):
-            self.reduce(chain, step)
+    def reduce_all(self, step, jobs=()):
+        self.events(self.reduce, step, jobs)
+
+    def events(self, action, step, jobs):
+        jobs = list(jobs)
+        for chain, (_, _, hops) in enumerate(self.chains):
+            if step < hops:
+                action(chain, step)
+                if jobs:
+                    jobs.pop(0)()
+        for job in jobs:
+            job()
 
     def total(self, half):
-        value = self.part(self.here, half)[...]
+        value = self.part(0, half)[...]
         for chain, (_, h, hops) in enumerate(self.chains):
             if h == half:
                 self.last[chain].wait_recv()
@@ -220,9 +250,8 @@
             if h == half:
                 self.gather(chain, 0)
 
-    def gather_all(self, step):
-        for chain in range(len(self.chains)):
-            self.gather(chain, step)
+    def gather_all(self, step, jobs=()):
+        self.events(self.gather, step, jobs)
 
     def arrived(self):
         for copy in self.last.values():
@@ -238,10 +267,10 @@
 
 
 def z_ring(net, part, slots, out):
-    rows, cols = part.shape[0] // NZ, part.shape[1] // 2
+    rows, cols = part.shape[0] // NZ, part.shape[1] // PARTS
 
     def block(ref):
-        return lambda owner, half: ref.at[at(owner * rows, rows), half * cols:(half + 1) * cols]
+        return lambda owner, half: ref.at[net.span("z", owner, rows), half * cols:(half + 1) * cols]
 
     ring = Ring(net, "z", Z_CHAINS, block(part), lambda chain, step: slots.at[slot_index(Z_CHAINS, chain, step)], block(out))
     ring.block = block
@@ -254,10 +283,10 @@
         half_rows = part.shape[2] // 2
 
         def block(ref):
-            return lambda owner, half: ref.at[owner, net.c, half * half_rows:(half + 1) * half_rows]
+            return lambda owner, half: ref.at[net.near("x", owner), net.c, half * half_rows:(half + 1) * half_rows]
 
         self.ring = Ring(net, "x", X_CHAINS, block(part), lambda chain, step: slots.at[slot_index(X_CHAINS, chain, step)], block(out))
-        self.swap = net.copy(part.at[:, 1 - net.c], sib, other_core=True)
+        self.swap = net.copy(part.at[:, net.other], sib, other_core=True)
         self.across, self.local = [], []
 
     def merge(self):
@@ -278,7 +307,7 @@
 
     def settle(self):
         for half in (0, 1):
-            own = self.ring.part(self.net.x, half)
+            own = self.ring.part(0, half)
             own[...] = self.ring.total(half)
             for chain, (_, h, _) in enumerate(X_CHAINS):
                 if h == half:
@@ -294,7 +323,7 @@
     def finish(self):
         self.ring.arrived()
         for dx in (1, -1, 2):
-            held = self.out.at[shift(self.net.x, dx, NX), self.net.c]
+            held = self.out.at[self.net.near("x", dx), self.net.c]
             self.cross(held, held)
         self.local.wait()
         self.swap.wait_send()
@@ -313,20 +342,20 @@
 
 def step_kernel(layers, total_tokens, *refs):
     refs = list(refs)
-    h0_ref, t_ref, w_up, w_down, x_all = take(refs, 5)
+    x_all, t_all, w_up, w_down = take(refs, 4)
     grad_up, grad_down = take(refs, 2)
     all_up, all_down, h_all, a_all, g_all, du_all = take(refs, 6)
     wu, wd, rows_buf, u_buf, act, dpre, part, slots = take(refs, 8)
     held_up, held_down = take(refs, 2)
     up_part, up_sib, up_slots, down_part, down_sib, down_slots = take(refs, 6)
-    a_in, g_in, h_in, du_in = take(refs, 4)
+    a_in, g_in, h_in, du_in, g_last, t_buf = take(refs, 6)
     net = Net(*refs)
     top = layers - 1
     width, hidden = wu.shape[1], wu.shape[2]
     cols = hidden // NY
     piece = held_up.shape[2]
     tile = width // 8
-    dp = net.x * 2 + net.c
+    pieces_at = {dx: at(net.block(dx) * piece, piece) for dx in range(NX)}
 
     def start(copies):
         for copy in copies:
@@ -336,19 +365,19 @@
         for copy in copies:
             copy.wait()
 
+    own_piece = pieces_at[0]
+
     def fetch_of(layer):
-        return (PieceFetch(net, w_up.at[layer, at(dp * piece, piece)], lambda slot: held_up.at[layer, slot]),
-                PieceFetch(net, w_down.at[layer, :, at(dp * piece, piece)], lambda slot: held_down.at[layer, slot * cols:(slot + 1) * cols]))
+        return (PieceFetch(net, w_up.at[layer, own_piece], lambda slot: held_up.at[layer, slot]),
+                PieceFetch(net, w_down.at[layer, :, own_piece], lambda slot: held_down.at[layer, slot * cols:(slot + 1) * cols]))
 
     def spread_of(layer):
         def up_view(dx, half):
-            first = (shift(net.x, dx, NX) * 2 + net.c) * piece
-            if half is None:
-                return all_up.at[layer, :, at(first, piece)]
-            return all_up.at[layer, :, at(first + half * (piece // 2), piece // 2)]
+            whole = all_up.at[layer, :, pieces_at[dx % NX]]
+            return whole if half is None else whole.at[:, half * (piece // 2):(half + 1) * (piece // 2)]
 
         def down_view(dx, half):
-            index, tall = shift(net.x, dx, NX) * 2 + net.c, 3 * cols
+            index, tall = net.block(dx), 3 * cols
             if half is None:
                 return all_down.at[layer, index]
             return all_down.at[layer, index, half * (tall // 2):(half + 1) * (tall // 2)]
@@ -373,8 +402,11 @@
     loads = up_loads(0), down_loads(0)
     loads[0][0].start()
     loads[1][0].start()
-    first = net.local(h0_ref, rows_buf.at[0])
-    first.start()
+    n_rows = rows_buf.shape[1]
+    n_slice = n_rows // NZ
+    first = [net.local(x_all.at[at(net.y * n_rows, n_rows)], rows_buf.at[0]),
+             net.local(t_all.at[at(net.y * n_rows + net.z * n_slice, n_slice)], t_buf)]
+    start(first)
     spread_up, spread_down = spread_of(0)
     fetches[0][0].arrived()
     spread_up.start()
@@ -385,15 +417,16 @@
     spread_up.cross()
     spread_up.finish()
     start(loads[0][1])
-    first.wait()
-
-    rows = None
+    wait(first)
+    per_part = 8 // PARTS
+
+    h_rows, a_moves = {}, []
     for layer in range(layers):
         b = layer % 2
         h_ref, out_ref = rows_buf.at[b], rows_buf.at[1 - b]
-        spreads = None
+        spreads, rows = None, None
         if layer > 0:
-            rows = RowGather(net, h_ref, h_all.at[layer - 1])
+            rows = h_rows[layer] = RowGather(net, h_ref, h_all.at[layer - 1])
             rows.start()
             if layer < top:
                 fetches[layer + 1][0].arrived()
@@ -411,6 +444,7 @@
             act[:, block] = gelu_tanh(pre.astype(F32)).astype(BF16)
 
         exchange = ColumnExchange(net, act, a_all.at[layer])
+        a_moves.append(exchange)
         if layer == 0:
             exchange.start()
             spread_down.cross()
@@ -427,10 +461,9 @@
 
         loads[1][0].wait()
         wait(loads[1][1])
-        pl.loop(0, 4)(down)
-        ring.reduce_half(0)
-        pl.loop(4, 8)(down)
-        ring.reduce_half(1)
+        for q in range(PARTS):
+            pl.loop(q * per_part, (q + 1) * per_part)(down)
+            ring.reduce_half(q)
         if layer == 0:
             for ahead in range(2, layers):
                 fetches.append(fetch_of(ahead))
@@ -439,20 +472,23 @@
             exchange.start()
         for step in (1, 2, 3):
             ring.reduce_all(step)
-        for half in (0, 1):
-            value = ring.block(h_ref)(net.z, half)[...] + ring.total(half).astype(BF16)
+        if spreads and layer > 0:
+            spreads[0].relay()
+            spreads[1].relay()
+        for q in range(PARTS):
+            value = ring.block(h_ref)(0, q)[...] + ring.total(q).astype(BF16)
             if layer == top:
                 wide = value.shape[1]
-                err = value.astype(F32) - t_ref[:, half * wide:(half + 1) * wide].astype(F32)
+                err = value.astype(F32) - t_buf[:, q * wide:(q + 1) * wide].astype(F32)
                 value = (err / total_tokens).astype(BF16)
-            ring.out(net.z, half)[...] = value
-            ring.gather_half(half)
-        if spreads:
+            ring.out(0, q)[...] = value
+            ring.gather_half(q)
+        if rows:
+            rows.relay()
+        if spreads and layer == 0:
             spreads[0].relay()
             spreads[1].relay()
         ring.gather_all(1)
-        if layer > 0:
-            rows.relay()
         ring.gather_all(2)
         if spreads:
             spreads[0].cross()
@@ -465,43 +501,45 @@
             for own, others in loads:
                 own.start()
                 start(others)
-        if layer > 0:
+        if rows:
             rows.sent()
-        exchange.finish()
+        exchange.sent()
         ring.arrived()
         ring.finish()
-        if layer > 0:
-            rows.finish()
     for pair in fetches:
         pair[0].sent()
         pair[1].sent()
 
-    def up_product():
+    def up_product(lo, hi):
         tall = up_part.shape[2]
 
-        @pl.loop(0, 2 * NX)
+        @pl.loop(lo, hi)
         def _(n):
             up_part[lax.div(n, 2), lax.rem(n, 2)] = lax.dot_general(
                 h_in[:, at(n * tall, tall)], du_in[...], ROW_CONTRACT, preferred_element_type=F32)
 
-    def down_product():
-        @pl.loop(0, 8)
+    def down_product(lo, hi, g):
+        @pl.loop(lo, hi)
         def _(n):
             block = at(n * tile, tile)
-            value = lax.dot_general(a_in[...], g_in[:, block], ROW_CONTRACT, preferred_element_type=F32)
+            value = lax.dot_general(a_in[...], g[:, block], ROW_CONTRACT, preferred_element_type=F32)
             down_part[:, :, :, block] = value.reshape(NX, 2, cols // 8, tile)
 
-    def up_sum_of(layer):
-        return GradSum(net, up_part, up_sib, up_slots, grad_up.at[layer])
-
-    def down_sum_of(layer):
-        return GradSum(net, down_part, down_sib, down_slots, grad_down.at[layer])
-
-    reload, last_rows, last_up = {}, None, None
+    def do(*actions):
+        def job():
+            for action in actions:
+                action()
+        return job
+
+    reload, prev_rows, prev_up, prev_down, prev_a, prev_layer = {}, None, None, None, None, None
     for layer in reversed(range(layers)):
         b = layer % 2
         g_ref, out_ref = rows_buf.at[1 - b], rows_buf.at[b]
+        if layer > 0:
+            h_rows[layer].finish()
+        a_moves[layer].arrived()
         h_load = net.local(x_all if layer == 0 else h_all.at[layer - 1], h_in)
+        h_load.start()
         a_load = net.local(a_all.at[layer], a_in)
         if layer in reload:
             reload[layer][0][0].wait()
@@ -515,123 +553,159 @@
             dpre[:, block] = gelu_vjp(d_act)[0].astype(BF16)
 
         exchange = ColumnExchange(net, dpre, du_all.at[layer])
+        exchange.start()
+        du_load = net.local(du_all.at[layer], du_in)
+        if layer == 0:
+            break
         rows = RowGather(net, g_ref, g_all.at[layer])
-        ring = None
-        if layer == 0:
-            exchange.start()
-            rows.start()
-        else:
-            if layer in reload:
-                reload[layer][1][0].wait()
-                wait(reload[layer][1][1])
-            ring = z_ring(net, part, slots, out_ref)
-
-            def back(n):
-                part[:, at(n * tile, tile)] = lax.dot_general(
-                    dpre[...], wu[b, at(n * tile, tile), :], COL_CONTRACT, preferred_element_type=F32)
-
-            pl.loop(0, 4)(back)
-            ring.reduce_half(0)
-            exchange.start()
-            rows.start()
-            pl.loop(4, 8)(back)
-            ring.reduce_half(1)
-        down_sum = None
-        if last_rows is not None:
-            last_rows.finish()
-            g_load = net.local(g_all.at[layer + 1], g_in)
-            g_load.start()
-            last_up.relay()
+        rows.start()
+        if layer in reload:
+            reload[layer][1][0].wait()
+            wait(reload[layer][1][1])
+        ring = z_ring(net, part, slots, out_ref)
+
+        def back(n):
+            part[:, at(n * tile, tile)] = lax.dot_general(
+                dpre[...], wu[b, at(n * tile, tile), :], COL_CONTRACT, preferred_element_type=F32)
+
+        for q in range(PARTS):
+            pl.loop(q * per_part, (q + 1) * per_part)(back)
+            ring.reduce_half(q)
         if layer >= 2:
             reload[layer - 2] = (down_loads(layer - 2), up_loads(layer - 2)) if layer > 2 else (down_loads(0),)
             for own, others in reload[layer - 2]:
                 own.start()
                 start(others)
-        if last_rows is not None:
-            g_load.wait()
-            last_a.wait()
-            down_sum = down_sum_of(layer + 1)
-            down_product()
-            down_sum.swap.start()
-        a_load.start()
-        h_load.start()
-        if ring:
-            ring.reduce_all(1)
+        jobs = {name: [] for name in ("r1", "r2", "r3", "t", "g1", "g2", "g3")}
+        up_sum = GradSum(net, up_part, up_sib, up_slots, grad_up.at[layer])
+        down_sum = None
+        if prev_down:
+            jobs["r1"] += [prev_down.relay]
+        if prev_up:
+            jobs["r1"] += [prev_up.step]
+        if prev_down:
+            jobs["r2"] += [do(prev_down.finish, prev_down.end)]
+        if prev_rows:
+            down_sum = GradSum(net, down_part, down_sib, down_slots, grad_down.at[prev_layer])
+            g_load = net.local(g_all.at[prev_layer], g_in)
+            jobs["r1"] += [do(prev_rows.finish, g_load.start)]
+            jobs["r2"] += [do(g_load.wait, prev_a.wait, functools.partial(down_product, 0, 2, g_in))]
+            jobs["r2"] += [functools.partial(down_product, n, n + 2, g_in) for n in (2, 4)]
+            jobs["r2"] += [do(functools.partial(down_product, 6, 8, g_in), down_sum.swap.start, a_load.start), prev_up.settle]
+            jobs["r3"] += [down_sum.merge, prev_up.relay]
+            jobs["t"] += [prev_up.finish]
+            jobs["g1"] += [do(prev_up.end, down_sum.step)]
+        else:
+            jobs["r2"] += [a_load.start]
+        jobs["r3"] += [do(exchange.sent, exchange.arrived, du_load.start)]
+        jobs["g1"] += [do(h_load.wait, du_load.wait, functools.partial(up_product, 0, 2))]
+        jobs["g1"] += [functools.partial(up_product, n, n + 2) for n in (2, 4)]
+        jobs["g1"] += [do(functools.partial(up_product, 6, 8), up_sum.swap.start)]
+        jobs["g2"] += [rows.relay, up_sum.merge]
         if down_sum:
-            last_up.finish()
-            down_sum.merge()
-        if ring:
-            ring.reduce_all(2)
-        if down_sum:
-            last_up.end()
-        exchange.finish()
-        du_load = net.local(du_all.at[layer], du_in)
-        du_load.start()
-        h_load.wait()
-        du_load.wait()
-        up_sum = up_sum_of(layer)
-        up_product()
-        up_sum.swap.start()
-        if ring:
-            ring.reduce_all(3)
-        if down_sum:
-            down_sum.step()
-        if ring:
-            for half in (0, 1):
-                total = ring.total(half)
-                ring.out(net.z, half)[...] = (ring.block(g_ref)(net.z, half)[...].astype(F32) + total).astype(BF16)
-                ring.gather_half(half)
-        up_sum.merge()
-        if ring:
-            ring.gather_all(1)
-        rows.relay()
-        if down_sum:
-            down_sum.settle()
-        if ring:
-            ring.gather_all(2)
-        up_sum.step()
-        if ring:
-            ring.gather_all(3)
+            jobs["g3"] += [down_sum.settle]
+        ring.reduce_all(1, jobs["r1"])
+        ring.reduce_all(2, jobs["r2"])
+        ring.reduce_all(3, jobs["r3"])
+        for q in range(PARTS):
+            total = ring.total(q)
+            ring.out(0, q)[...] = (ring.block(g_ref)(0, q)[...].astype(F32) + total).astype(BF16)
+            ring.gather_half(q)
+        for job in jobs["t"]:
+            job()
+        ring.gather_all(1, jobs["g1"])
+        ring.gather_all(2, jobs["g2"])
+        ring.gather_all(3, jobs["g3"])
         rows.sent()
-        if down_sum:
-            down_sum.relay()
-        if ring:
-            ring.arrived()
-            ring.finish()
-        if layer > 0:
-            up_sum.settle()
-        if down_sum:
-            down_sum.finish()
-            down_sum.end()
-        last_rows, last_up, last_a = rows, up_sum, a_load
-    last_up.settle()
-    last_rows.finish()
-    g_load = net.local(g_all.at[0], g_in)
+        ring.arrived()
+        ring.finish()
+        prev_rows, prev_up, prev_down, prev_a, prev_layer = rows, up_sum, down_sum, a_load, layer
+
+    wide = width // PARTS
+
+    def piece_of(ref, q):
+        return ref.at[(slice(None),) * (len(ref.shape) - 1) + (slice(q * wide, (q + 1) * wide),)]
+
+    pieces = [RowGather(net, piece_of(g_ref, q), piece_of(g_last, q)) for q in range(PARTS)]
+    pieces[0].start()
+    pieces[1].start()
+    if prev_down:
+        prev_down.relay()
+    prev_up.step()
+    prev_rows.finish()
+    g_load = net.local(g_all.at[prev_layer], g_in)
     g_load.start()
-    last_up.relay()
+    if prev_down:
+        prev_down.finish()
+        prev_down.end()
     g_load.wait()
-    last_a.wait()
-    down_sum = down_sum_of(0)
-    down_product()
+    prev_a.wait()
+    down_sum = GradSum(net, down_part, down_sib, down_slots, grad_down.at[prev_layer])
+    down_product(0, 8, g_in)
     down_sum.swap.start()
-    last_up.finish()
+    a_load.start()
+    prev_up.settle()
+    exchange.sent()
+    exchange.arrived()
+    du_load.start()
     down_sum.merge()
+    prev_up.relay()
+    pieces[0].relay()
+    pieces[2].start()
+    prev_up.finish()
     down_sum.step()
+    prev_up.end()
+    h_load.wait()
+    du_load.wait()
+    up_sum = GradSum(net, up_part, up_sib, up_slots, grad_up.at[0])
+    up_product(0, 8)
+    up_sum.swap.start()
+    pieces[1].relay()
+    pieces[3].start()
+    up_sum.merge()
     down_sum.settle()
+    pieces[2].relay()
+    up_sum.step()
     down_sum.relay()
-    last_up.end()
+    pieces[3].relay()
+    up_sum.settle()
     down_sum.finish()
     down_sum.end()
+    a_load.wait()
+    sums = []
+    for q in range(PARTS):
+        pieces[q].sent()
+        pieces[q].finish()
+        down_product(q * per_part, (q + 1) * per_part, g_last)
+        sums.append(GradSum(net, piece_of(down_part, q), piece_of(down_sib, q), piece_of(down_slots, q), piece_of(grad_down.at[0], q)))
+        sums[q].swap.start()
+        if q == 1:
+            up_sum.relay()
+        if q == 2:
+            sums[0].step()
+        sums[q].merge()
+    up_sum.finish()
+    sums[1].step()
+    sums[0].settle()
+    sums[2].step()
+    sums[1].settle()
+    sums[3].step()
+    sums[2].settle()
+    sums[0].relay()
+    sums[3].settle()
+    for q in (1, 2, 3):
+        sums[q].relay()
+    up_sum.end()
+    for q in range(PARTS):
+        sums[q].finish()
+    for q in range(PARTS):
+        sums[q].end()
 
 
 def local_step(hidden, targets, w_up, w_down, n_dp):
     layers, width, cols = w_up.shape
     tokens = hidden.shape[0]
     rows, inner, piece = tokens // NY, cols * NY, width // n_dp
-    tp = lax.axis_index("tp")
-    z, y = lax.div(tp, NY), lax.rem(tp, NY)
-    h_own = lax.dynamic_slice(hidden, (y * rows, 0), (rows, width))
-    t_own = lax.dynamic_slice(targets, (y * rows + z * (rows // NZ), 0), (rows // NZ, width))
     up_shape, down_shape = (NX, 2, width // 8, cols), (NX, 2, cols // 8, width)
 
     def out(dtype, *shape):
@@ -647,16 +721,17 @@
 
     scratch = [pltpu.VMEM((2, width, inner), BF16), pltpu.VMEM((2, inner, width), BF16), pltpu.VMEM((2, rows, width), BF16),
                pltpu.VMEM((layers, rows, inner), BF16), pltpu.VMEM((rows, inner), BF16), pltpu.VMEM((rows, inner), BF16),
-               pltpu.VMEM((rows, width), F32), pltpu.VMEM((14, rows // NZ, width // 2), F32),
+               pltpu.VMEM((rows, width), F32), pltpu.VMEM((7 * PARTS, rows // NZ, width // PARTS), F32),
                pltpu.VMEM((layers, NY - 1, piece, cols), BF16), pltpu.VMEM((layers, (NY - 1) * cols, piece), BF16),
                *sum_scratch(up_shape), *sum_scratch(down_shape),
                pltpu.VMEM((tokens, cols), BF16), pltpu.VMEM((tokens, width), BF16), pltpu.VMEM((tokens, width), BF16), pltpu.VMEM((tokens, cols), BF16),
+               pltpu.VMEM((tokens, width), BF16), pltpu.VMEM((rows // NZ, width), BF16),
                pltpu.SemaphoreType.DMA((COPIES,)), pltpu.SemaphoreType.DMA((COPIES,)), pltpu.SemaphoreType.DMA((LOCALS,))]
     up, down = pl.pallas_call(
-        functools.partial(step_kernel, layers, tokens * n_dp), out_shape=outs, in_specs=[ANY, VMEM, ANY, ANY, ANY],
+        functools.partial(step_kernel, layers, tokens * n_dp), out_shape=outs, in_specs=[ANY] * 4,
         out_specs=[ANY] * len(outs), scratch_shapes=scratch, name="step",
         compiler_params=pltpu.CompilerParams(collective_id=0, has_side_effects=True, vmem_limit_bytes=60 * 1024 * 1024),
-    )(h_own, t_own, w_up, w_down, hidden)[:2]
+    )(hidden, targets, w_up, w_down)[:2]
     return up.reshape(layers, width, cols), down.reshape(layers, cols, width)
 
 

time: 474 us -> 460 us (0.970)
  Pallas kernels: 458 us -> 448 us
    pallas_call x1, Pallas kernels: 458 us -> 448 us  [local_step(): pl.pallas_call(functools.partial(step_kernel, layers, tokens * n_dp), out...]
where the time goes in v4:
time: 460 us
  Pallas kernels  448 us (97%)
  local copies, waits for them, and re-layouts  11.1 us (2%)
    pallas_call x1, Pallas kernels, local_step(): pl.pallas_call(functools.partial(step_kernel, layers, tokens * n_dp), out...  448 us
    unnamed x4, local copies, waits for them, and re-layouts  11.1 us

profile of v4, /device:TPU:1, one launch (start us, length us, event | category | flops | bytes accessed | tf_op | source)
XLA Modules:
  0.0 459.9 jit_solution(17989983056352487238)
XLA Ops:
  0.6 448.2 %step.1 = (f32[4,4,2,256,256]{4,3,2,1,0:T(8,128)}, f32[4,4,2,32,2048]{4,3,2,1,0:T(8,128)}, bf16[4,3,2048,256]{3,2,1,0:T(8,128)(2,1)}, bf16[4,8,768,256]{3,2,1,0:...) custom-call(bf16[1024,2048]{1,0:T(8,128)(2,1)} %refs_0_.1, ...), custom_call_target="tpu_custom_call" | custom-call | tf_op jit(solution)/shard_map/step/pallas_call | solution.py:730
  448.8 0.0 copy-start
  448.8 7.7 %copy.8 = f32[4,2048,256]{2,1,0:T(8,128)} copy(f32[4,2048,256]{2,1,0:T(8,128)} %bitcast.3) | data formatting | bytes 16777216
  456.5 0.0 copy-done
  456.5 3.4 copy.9
Async XLA Ops:
  448.8 7.7 %copy-start = (f32[4,4,2,32,2048]{4,3,2,1,0:T(8,128)S(1)}, f32[4,4,2,32,2048]{4,3,2,1,0:T(8,128)}, u32[]{:S(2)}) copy-start(f32[4,4,2,32,2048]{4,3,2,1,0:T(8,128)} %get-tuple-element.5) | copy-start | bytes 25165828

commit v5 on v4

--- a/solution.py
+++ b/solution.py
@@ -397,8 +397,9 @@
     net.barrier()
     fetches = [fetch_of(0)]
     start(fetches[0])
-    fetches.append(fetch_of(1))
-    start(fetches[1])
+    for ahead in range(1, layers - 1):
+        fetches.append(fetch_of(ahead))
+        start(fetches[ahead])
     loads = up_loads(0), down_loads(0)
     loads[0][0].start()
     loads[1][0].start()
@@ -465,9 +466,8 @@
             pl.loop(q * per_part, (q + 1) * per_part)(down)
             ring.reduce_half(q)
         if layer == 0:
-            for ahead in range(2, layers):
-                fetches.append(fetch_of(ahead))
-                start(fetches[ahead])
+            fetches.append(fetch_of(top))
+            start(fetches[top])
         else:
             exchange.start()
         for step in (1, 2, 3):
@@ -531,6 +531,10 @@
                 action()
         return job
 
+    def piece_of(ref, q, count=PARTS):
+        wide = ref.shape[-1] // count
+        return ref.at[(slice(None),) * (len(ref.shape) - 1) + (slice(q * wide, (q + 1) * wide),)]
+
     reload, prev_rows, prev_up, prev_down, prev_a, prev_layer = {}, None, None, None, None, None
     for layer in reversed(range(layers)):
         b = layer % 2
@@ -557,8 +561,9 @@
         du_load = net.local(du_all.at[layer], du_in)
         if layer == 0:
             break
-        rows = RowGather(net, g_ref, g_all.at[layer])
-        rows.start()
+        rows = [RowGather(net, piece_of(g_ref, k, 2), piece_of(g_all.at[layer], k, 2)) for k in (0, 1)]
+        for gather in rows:
+            gather.start()
         if layer in reload:
             reload[layer][1][0].wait()
             wait(reload[layer][1][1])
@@ -581,29 +586,29 @@
         down_sum = None
         if prev_down:
             jobs["r1"] += [prev_down.relay]
-        if prev_up:
-            jobs["r1"] += [prev_up.step]
-        if prev_down:
-            jobs["r2"] += [do(prev_down.finish, prev_down.end)]
         if prev_rows:
             down_sum = GradSum(net, down_part, down_sib, down_slots, grad_down.at[prev_layer])
             g_load = net.local(g_all.at[prev_layer], g_in)
-            jobs["r1"] += [do(prev_rows.finish, g_load.start)]
+            jobs["r1"] += [prev_up.settle, do(prev_rows[0].finish, prev_rows[1].finish, g_load.start)]
+            if prev_down:
+                jobs["r2"] += [do(prev_down.finish, prev_down.end)]
             jobs["r2"] += [do(g_load.wait, prev_a.wait, functools.partial(down_product, 0, 2, g_in))]
             jobs["r2"] += [functools.partial(down_product, n, n + 2, g_in) for n in (2, 4)]
-            jobs["r2"] += [do(functools.partial(down_product, 6, 8, g_in), down_sum.swap.start, a_load.start), prev_up.settle]
-            jobs["r3"] += [down_sum.merge, prev_up.relay]
-            jobs["t"] += [prev_up.finish]
-            jobs["g1"] += [do(prev_up.end, down_sum.step)]
+            jobs["r2"] += [do(functools.partial(down_product, 6, 8, g_in), down_sum.swap.start, a_load.start), prev_up.relay]
         else:
             jobs["r2"] += [a_load.start]
         jobs["r3"] += [do(exchange.sent, exchange.arrived, du_load.start)]
-        jobs["g1"] += [do(h_load.wait, du_load.wait, functools.partial(up_product, 0, 2))]
-        jobs["g1"] += [functools.partial(up_product, n, n + 2) for n in (2, 4)]
-        jobs["g1"] += [do(functools.partial(up_product, 6, 8), up_sum.swap.start)]
-        jobs["g2"] += [rows.relay, up_sum.merge]
+        if prev_rows:
+            jobs["r3"] += [down_sum.merge, prev_up.finish]
+            jobs["t"] += [prev_up.end]
+        jobs["t"] += [do(h_load.wait, du_load.wait, functools.partial(up_product, 0, 2))]
+        jobs["t"] += [functools.partial(up_product, n, n + 2) for n in (2, 4)]
+        jobs["t"] += [do(functools.partial(up_product, 6, 8), up_sum.swap.start), rows[0].relay]
+        jobs["g1"] += [up_sum.merge]
         if down_sum:
+            jobs["g1"] += [down_sum.step]
             jobs["g3"] += [down_sum.settle]
+        jobs["g3"] += [up_sum.step]
         ring.reduce_all(1, jobs["r1"])
         ring.reduce_all(2, jobs["r2"])
         ring.reduce_all(3, jobs["r3"])
@@ -611,28 +616,28 @@
             total = ring.total(q)
             ring.out(0, q)[...] = (ring.block(g_ref)(0, q)[...].astype(F32) + total).astype(BF16)
             ring.gather_half(q)
+            if q + 1 < PARTS:
+                jobs["t"].pop(0)()
         for job in jobs["t"]:
             job()
         ring.gather_all(1, jobs["g1"])
         ring.gather_all(2, jobs["g2"])
         ring.gather_all(3, jobs["g3"])
-        rows.sent()
+        rows[1].relay()
+        for gather in rows:
+            gather.sent()
         ring.arrived()
         ring.finish()
         prev_rows, prev_up, prev_down, prev_a, prev_layer = rows, up_sum, down_sum, a_load, layer
-
-    wide = width // PARTS
-
-    def piece_of(ref, q):
-        return ref.at[(slice(None),) * (len(ref.shape) - 1) + (slice(q * wide, (q + 1) * wide),)]
 
     pieces = [RowGather(net, piece_of(g_ref, q), piece_of(g_last, q)) for q in range(PARTS)]
     pieces[0].start()
     pieces[1].start()
     if prev_down:
         prev_down.relay()
-    prev_up.step()
-    prev_rows.finish()
+    prev_up.settle()
+    for gather in prev_rows:
+        gather.finish()
     g_load = net.local(g_all.at[prev_layer], g_in)
     g_load.start()
     if prev_down:
@@ -644,22 +649,21 @@
     down_product(0, 8, g_in)
     down_sum.swap.start()
     a_load.start()
-    prev_up.settle()
+    prev_up.relay()
     exchange.sent()
     exchange.arrived()
     du_load.start()
     down_sum.merge()
-    prev_up.relay()
     pieces[0].relay()
     pieces[2].start()
     prev_up.finish()
-    down_sum.step()
     prev_up.end()
     h_load.wait()
     du_load.wait()
     up_sum = GradSum(net, up_part, up_sib, up_slots, grad_up.at[0])
     up_product(0, 8)
     up_sum.swap.start()
+    down_sum.step()
     pieces[1].relay()
     pieces[3].start()
     up_sum.merge()

time: 460 us -> 444 us (0.965)
  Pallas kernels: 448 us -> 432 us
    pallas_call x1, Pallas kernels: 448 us -> 432 us  [local_step(): pl.pallas_call(functools.partial(step_kernel, layers, tokens * n_dp), out...]
where the time goes in v5:
time: 444 us
  Pallas kernels  432 us (97%)
  local copies, waits for them, and re-layouts  11.1 us (2%)
    pallas_call x1, Pallas kernels, local_step(): pl.pallas_call(functools.partial(step_kernel, layers, tokens * n_dp), out...  432 us
    unnamed x4, local copies, waits for them, and re-layouts  11.1 us

profile of v5, /device:TPU:1, one launch (start us, length us, event | category | flops | bytes accessed | tf_op | source)
XLA Modules:
  0.0 443.6 jit_solution(3547568138355930674)
XLA Ops:
  0.6 431.9 %step.1 = (f32[4,4,2,256,256]{4,3,2,1,0:T(8,128)}, f32[4,4,2,32,2048]{4,3,2,1,0:T(8,128)}, bf16[4,3,2048,256]{3,2,1,0:T(8,128)(2,1)}, bf16[4,8,768,256]{3,2,1,0:...) custom-call(bf16[1024,2048]{1,0:T(8,128)(2,1)} %refs_0_.1, ...), custom_call_target="tpu_custom_call" | custom-call | tf_op jit(solution)/shard_map/step/pallas_call | solution.py:734
  432.6 0.0 copy-start
  432.6 7.7 %copy.8 = f32[4,2048,256]{2,1,0:T(8,128)} copy(f32[4,2048,256]{2,1,0:T(8,128)} %bitcast.3) | data formatting | bytes 16777216
  440.2 0.0 copy-done
  440.2 3.4 copy.9
Async XLA Ops:
  432.6 7.7 %copy-start = (f32[4,4,2,32,2048]{4,3,2,1,0:T(8,128)S(1)}, f32[4,4,2,32,2048]{4,3,2,1,0:T(8,128)}, u32[]{:S(2)}) copy-start(f32[4,4,2,32,2048]{4,3,2,1,0:T(8,128)} %get-tuple-element.5) | copy-start | bytes 25165828

commit v6 on v5

--- a/solution.py
+++ b/solution.py
@@ -545,6 +545,9 @@
         h_load = net.local(x_all if layer == 0 else h_all.at[layer - 1], h_in)
         h_load.start()
         a_load = net.local(a_all.at[layer], a_in)
+        if layer == 0:
+            pieces = [RowGather(net, piece_of(g_ref, q), piece_of(g_last, q)) for q in range(PARTS)]
+            pieces[0].start()
         if layer in reload:
             reload[layer][0][0].wait()
             wait(reload[layer][0][1])
@@ -630,8 +633,6 @@
         ring.finish()
         prev_rows, prev_up, prev_down, prev_a, prev_layer = rows, up_sum, down_sum, a_load, layer
 
-    pieces = [RowGather(net, piece_of(g_ref, q), piece_of(g_last, q)) for q in range(PARTS)]
-    pieces[0].start()
     pieces[1].start()
     if prev_down:
         prev_down.relay()

time: 444 us -> 444 us (level)
  no operation moved by 1% of the time
where the time goes in v6:
time: 444 us
  Pallas kernels  432 us (97%)
  local copies, waits for them, and re-layouts  11.1 us (2%)
    pallas_call x1, Pallas kernels, local_step(): pl.pallas_call(functools.partial(step_kernel, layers, tokens * n_dp), out...  432 us
    unnamed x4, local copies, waits for them, and re-layouts  11.1 us

profile of v6, /device:TPU:1, one launch (start us, length us, event | category | flops | bytes accessed | tf_op | source)
XLA Modules:
  0.0 443.6 jit_solution(4275599885508241121)
XLA Ops:
  0.6 431.9 %step.1 = (f32[4,4,2,256,256]{4,3,2,1,0:T(8,128)}, f32[4,4,2,32,2048]{4,3,2,1,0:T(8,128)}, bf16[4,3,2048,256]{3,2,1,0:T(8,128)(2,1)}, bf16[4,8,768,256]{3,2,1,0:...) custom-call(bf16[1024,2048]{1,0:T(8,128)(2,1)} %refs_0_.1, ...), custom_call_target="tpu_custom_call" | custom-call | tf_op jit(solution)/shard_map/step/pallas_call | solution.py:735
  432.6 0.0 copy-start
  432.6 7.7 %copy.8 = f32[4,2048,256]{2,1,0:T(8,128)} copy(f32[4,2048,256]{2,1,0:T(8,128)} %bitcast.3) | data formatting | bytes 16777216
  440.2 0.0 copy-done
  440.2 3.4 copy.9
Async XLA Ops:
  432.6 7.7 %copy-start = (f32[4,4,2,32,2048]{4,3,2,1,0:T(8,128)S(1)}, f32[4,4,2,32,2048]{4,3,2,1,0:T(8,128)}, u32[]{:S(2)}) copy-start(f32[4,4,2,32,2048]{4,3,2,1,0:T(8,128)} %get-tuple-element.5) | copy-start | bytes 25165828
